TPU v7x, 32 devices: a whole 2x2x4 slice. The times are simulated.
32 devices in a mesh: fsdp: 16 (over z, y, x), rep: 2 (over core).
Axes of the slice: x: 2, y: 2, z: 4, core: 2. Of those that a mesh axis runs over, the one named last changes fastest.
Arguments:
- captions: bfloat16 [320, 128, 768], P(('fsdp', 'rep')), may hold values from -6 to 6
- regions: bfloat16 [64, 128, 768], P(('fsdp', 'rep')), may hold values from -6 to 6
- caption_lengths: int32 [320], P(('fsdp', 'rep')), may hold values from 64 to 128, as said below
- region_counts: int32 [64], P(('fsdp', 'rep')), may hold values from 36 to 100, as said below
- group_ids: int32 [320], P(('fsdp', 'rep')), may hold values from 0 to 1, as said below
- query_weight: bfloat16 [768, 768], P('fsdp'), may hold values from -0.21875 to 0.21875
- key_weight: bfloat16 [768, 768], P('fsdp'), may hold values from -0.21875 to 0.21875
- value_weight: bfloat16 [768, 768], P('fsdp'), may hold values from -0.21875 to 0.21875
- out_weight: bfloat16 [768, 768], P('fsdp'), may hold values from -1.5 to 1.5
- query_bias: bfloat16 [768], P('fsdp'), may hold values from -3 to 3
- value_bias: bfloat16 [768], P('fsdp'), may hold values from -3 to 3
- out_bias: bfloat16 [768], P('fsdp'), may hold values from -3 to 3
- first_gain: bfloat16 [768], P('fsdp'), may hold values from 0.25 to 1.75
- first_shift: bfloat16 [768], P('fsdp'), may hold values from -3 to 3
- inner_weight: bfloat16 [768, 3072], P('fsdp'), may hold values from -0.21875 to 0.21875
- inner_bias: bfloat16 [3072], P('fsdp'), may hold values from -3 to 3
- outer_weight: bfloat16 [3072, 768], P('fsdp'), may hold values from -0.109375 to 0.109375
- outer_bias: bfloat16 [768], P('fsdp'), may hold values from -3 to 3
- second_gain: bfloat16 [768], P('fsdp'), may hold values from 0.25 to 1.75
- second_shift: bfloat16 [768], P('fsdp'), may hold values from -3 to 3
- caption_cotangent: bfloat16 [320, 128, 768], P(('fsdp', 'rep')), may hold values from -6 to 6
- region_cotangent: bfloat16 [320, 128, 768], P(('fsdp', 'rep')), may hold values from -6 to 6
Outputs:
- out_caption: bfloat16 [320, 128, 768], P(('fsdp', 'rep'))
- out_region: bfloat16 [320, 128, 768], P(('fsdp', 'rep'))
- grad_captions: float32 [320, 128, 768], P(('fsdp', 'rep'))
- grad_regions: float32 [64, 128, 768], P(('fsdp', 'rep'))
- query_weight_grad: float32 [768, 768], P('fsdp')
- key_weight_grad: float32 [768, 768], P('fsdp')
- value_weight_grad: float32 [768, 768], P('fsdp')
- out_weight_grad: float32 [768, 768], P('fsdp')
- query_bias_grad: float32 [768], P('fsdp')
- value_bias_grad: float32 [768], P('fsdp')
- out_bias_grad: float32 [768], P('fsdp')
- first_gain_grad: float32 [768], P('fsdp')
- first_shift_grad: float32 [768], P('fsdp')
- inner_weight_grad: float32 [768, 3072], P('fsdp')
- inner_bias_grad: float32 [3072], P('fsdp')
- outer_weight_grad: float32 [3072, 768], P('fsdp')
- outer_bias_grad: float32 [768], P('fsdp')
- second_gain_grad: float32 [768], P('fsdp')
- second_shift_grad: float32 [768], P('fsdp')
Inputs may be any that keep to these rules, and one draw needn't show every extreme that they name: `caption_lengths`: the slots of a caption past its length are padding; some caption reaches 128. `region_counts`: the slots of an image past its count are padding; some image reaches 100. Sequence s uses image (s // 10) * 2 + group_ids[s]; every image is used by exactly five sequences.
All inputs are finite; a program needn't handle non-finite values.
Results may differ from a plain program's by a relative error of at most 0.015.
Values may be sent and summed in bfloat16 or wider, within the bound.
A program may use at most 320 MiB of HBM per device.

v0:
```python
import jax
import jax.numpy as jnp
from jax import lax
from jax.sharding import PartitionSpec as P

HEADS = 12


EPSILON = 1e-12
MASKED_SCORE = -1e30
HIGHEST_PRECISION = lax.Precision.HIGHEST


def normalize(values, norm_gain, norm_shift):
    average = jnp.mean(values, axis=-1, keepdims=True)
    centred = values - average
    spread = jnp.mean(centred * centred, axis=-1, keepdims=True)
    return centred * lax.rsqrt(spread + EPSILON) * norm_gain + norm_shift


def exact_gelu(values):
    return jax.nn.gelu(values, approximate=False)


def forward_rows(row_block, weight):
    return jnp.dot(row_block, weight, preferred_element_type=jnp.float32)


def backward_rows(gradient, weight):
    return lax.dot_general(
        gradient, weight, (((1,), (1,)), ((), ())), preferred_element_type=jnp.float32
    )


def weight_grad(row_block, gradient):
    return lax.dot_general(
        row_block, gradient, (((0,), (0,)), ((), ())), preferred_element_type=jnp.float32
    )


def column_sum(gradient):
    return jnp.sum(gradient.astype(jnp.float32), axis=0)


def on_device(
    captions,
    regions,
    caption_lengths,
    region_counts,
    group_ids,
    query_weight,
    key_weight,
    value_weight,
    out_weight,
    query_bias,
    value_bias,
    out_bias,
    first_gain,
    first_shift,
    inner_weight,
    inner_bias,
    outer_weight,
    outer_bias,
    second_gain,
    second_shift,
    caption_cotangent,
    region_cotangent,
):
    seq_count = captions.shape[0]
    caption_slots = captions.shape[1]
    width_model = captions.shape[2]
    image_count = regions.shape[0]
    region_slots = regions.shape[1]
    row_length = caption_slots + region_slots
    head_count = HEADS
    head_size = width_model // head_count
    scaling = head_size ** (-0.5)
    all_rows = seq_count * row_length
    (
        query_all,
        key_all,
        value_all,
        out_all,
        query_offset,
        value_offset,
        out_offset,
        gain_first,
        shift_first,
    ) = (
        lax.all_gather(query_weight, "fsdp", axis=0, tiled=True),
        lax.all_gather(key_weight, "fsdp", axis=0, tiled=True),
        lax.all_gather(value_weight, "fsdp", axis=0, tiled=True),
        lax.all_gather(out_weight, "fsdp", axis=0, tiled=True),
        lax.all_gather(query_bias, "fsdp", axis=0, tiled=True),
        lax.all_gather(value_bias, "fsdp", axis=0, tiled=True),
        lax.all_gather(out_bias, "fsdp", axis=0, tiled=True),
        lax.all_gather(first_gain, "fsdp", axis=0, tiled=True),
        lax.all_gather(first_shift, "fsdp", axis=0, tiled=True),
    )
    image_match = group_ids[:, None] == jnp.arange(image_count, dtype=jnp.int32)[None, :]
    match_low = image_match.astype(jnp.bfloat16)
    match_float = image_match.astype(jnp.float32)
    seq_regions = jnp.sum(jnp.where(image_match, region_counts[None, :], 0), axis=1)
    caption_live = jnp.arange(caption_slots, dtype=jnp.int32)[None, :] < caption_lengths[:, None]
    region_live = jnp.arange(region_slots, dtype=jnp.int32)[None, :] < seq_regions[:, None]
    live_rows = jnp.concatenate([caption_live, region_live], axis=1)
    live_column = live_rows.reshape(all_rows, 1).astype(jnp.float32)

    def spread_images(table):
        spread_out = jnp.einsum("si,ird->srd", match_low, table, preferred_element_type=jnp.float32)
        return spread_out.astype(jnp.bfloat16)

    def collect_images(gradient):
        summed = jnp.einsum("si,srd->ird", match_float, gradient, precision=HIGHEST_PRECISION)
        return summed.reshape(image_count * region_slots, width_model)

    caption_flat = captions.reshape(seq_count * caption_slots, width_model)
    region_flat = regions.reshape(image_count * region_slots, width_model)

    def sequence_rows(caption_part, image_part):
        caption_block = caption_part.reshape(seq_count, caption_slots, width_model)
        image_block = spread_images(image_part.reshape(image_count, region_slots, width_model))
        joined = jnp.concatenate([caption_block, image_block], axis=1)
        return joined.reshape(seq_count, row_length, head_count, head_size)

    def project_three(row_block):
        query_rows = (forward_rows(row_block, query_all) + query_offset.astype(jnp.float32)).astype(
            jnp.bfloat16
        )
        key_rows = forward_rows(row_block, key_all).astype(jnp.bfloat16)
        value_rows = (forward_rows(row_block, value_all) + value_offset.astype(jnp.float32)).astype(
            jnp.bfloat16
        )
        return (query_rows, key_rows, value_rows)

    query_caption, key_caption, value_caption = project_three(caption_flat)
    query_image, key_image, value_image = project_three(region_flat)
    queries = sequence_rows(query_caption, query_image)
    keys_seq = sequence_rows(key_caption, key_image)
    values_seq = sequence_rows(value_caption, value_image)

    def masked_scores():
        products = (
            jnp.einsum("sqhe,skhe->shqk", queries, keys_seq, preferred_element_type=jnp.float32)
            * scaling
        )
        return jnp.where(live_rows[:, None, None, :], products, MASKED_SCORE)

    scores = masked_scores()
    row_max = jnp.max(scores, axis=-1, keepdims=True)
    log_total = row_max + jnp.log(jnp.sum(jnp.exp(scores - row_max), axis=-1, keepdims=True))
    probs_low = jnp.exp(scores - log_total).astype(jnp.bfloat16)
    context = jnp.einsum(
        "shqk,skhe->sqhe", probs_low, values_seq, preferred_element_type=jnp.float32
    )
    context = context.astype(jnp.bfloat16).reshape(all_rows, width_model)
    inputs_seq = jnp.concatenate([captions, spread_images(regions)], axis=1).reshape(
        all_rows, width_model
    )
    first_sum = (
        inputs_seq.astype(jnp.float32)
        + forward_rows(context, out_all)
        + out_offset.astype(jnp.float32)
    )
    first_out, first_back = jax.vjp(
        normalize, first_sum, gain_first.astype(jnp.float32), shift_first.astype(jnp.float32)
    )
    first_low = first_out.astype(jnp.bfloat16)
    inner_all, inner_offset, outer_all, outer_offset, gain_second, shift_second = (
        lax.all_gather(inner_weight, "fsdp", axis=0, tiled=True),
        lax.all_gather(inner_bias, "fsdp", axis=0, tiled=True),
        lax.all_gather(outer_weight, "fsdp", axis=0, tiled=True),
        lax.all_gather(outer_bias, "fsdp", axis=0, tiled=True),
        lax.all_gather(second_gain, "fsdp", axis=0, tiled=True),
        lax.all_gather(second_shift, "fsdp", axis=0, tiled=True),
    )
    inner_pre = forward_rows(first_low, inner_all) + inner_offset.astype(jnp.float32)
    active_low = exact_gelu(inner_pre).astype(jnp.bfloat16)
    second_sum = first_out + forward_rows(active_low, outer_all) + outer_offset.astype(jnp.float32)
    second_out, second_back = jax.vjp(
        normalize, second_sum, gain_second.astype(jnp.float32), shift_second.astype(jnp.float32)
    )
    layer_out = (second_out * live_column).reshape(seq_count, row_length, width_model)
    out_caption = layer_out[:, :caption_slots].astype(jnp.bfloat16)
    out_region = layer_out[:, caption_slots:].astype(jnp.bfloat16)
    cotangent = jnp.concatenate([caption_cotangent, region_cotangent], axis=1)
    cotangent = cotangent.reshape(all_rows, width_model).astype(jnp.float32) * live_column
    second_grad, second_gain_grad, second_shift_grad = second_back(cotangent)
    inner_back, outer_back = (inner_all, outer_all)
    outer_grad = second_grad.astype(jnp.bfloat16)
    outer_weight_grad = weight_grad(active_low, outer_grad)
    outer_bias_grad = column_sum(outer_grad)
    active_grad = backward_rows(outer_grad, outer_back)
    inner_grad = jax.vjp(exact_gelu, inner_pre)[1](active_grad)[0].astype(jnp.bfloat16)
    inner_weight_grad = weight_grad(first_low, inner_grad)
    inner_bias_grad = column_sum(inner_grad)
    first_grad = second_grad + backward_rows(inner_grad, inner_back)
    sum_grad, first_gain_grad, first_shift_grad = first_back(first_grad)
    query_back, key_back, value_back, out_back = (query_all, key_all, value_all, out_all)
    attended_grad = sum_grad.astype(jnp.bfloat16)
    out_weight_grad = weight_grad(context, attended_grad)
    out_bias_grad = column_sum(attended_grad)
    context_grad = backward_rows(attended_grad, out_back).astype(jnp.bfloat16)
    context_grad = context_grad.reshape(seq_count, row_length, head_count, head_size)
    scores_again = masked_scores()
    probs_again = jnp.exp(scores_again - log_total)
    probs_grad = jnp.einsum(
        "sqhe,skhe->shqk", context_grad, values_seq, preferred_element_type=jnp.float32
    )
    value_grad = jnp.einsum(
        "shqk,sqhe->skhe",
        probs_again.astype(jnp.bfloat16),
        context_grad,
        preferred_element_type=jnp.float32,
    )
    row_inner = jnp.sum(probs_grad * probs_again, axis=-1, keepdims=True)
    score_grad = (probs_again * (probs_grad - row_inner)).astype(jnp.bfloat16)
    query_grad = (
        jnp.einsum("shqk,skhe->sqhe", score_grad, keys_seq, preferred_element_type=jnp.float32)
        * scaling
    )
    key_grad = (
        jnp.einsum("shqk,sqhe->skhe", score_grad, queries, preferred_element_type=jnp.float32)
        * scaling
    )

    def split_grad(gradient):
        grid = gradient.reshape(seq_count, row_length, width_model)
        caption_part = grid[:, :caption_slots].reshape(seq_count * caption_slots, width_model)
        image_part = collect_images(grid[:, caption_slots:])
        return (caption_part.astype(jnp.bfloat16), image_part.astype(jnp.bfloat16))

    query_cap_grad, query_img_grad = split_grad(query_grad)
    key_cap_grad, key_img_grad = split_grad(key_grad)
    value_cap_grad, value_img_grad = split_grad(value_grad)
    query_weight_grad = weight_grad(caption_flat, query_cap_grad) + weight_grad(
        region_flat, query_img_grad
    )
    query_bias_grad = column_sum(query_cap_grad) + column_sum(query_img_grad)
    key_weight_grad = weight_grad(caption_flat, key_cap_grad) + weight_grad(
        region_flat, key_img_grad
    )
    value_weight_grad = weight_grad(caption_flat, value_cap_grad) + weight_grad(
        region_flat, value_img_grad
    )
    value_bias_grad = column_sum(value_cap_grad) + column_sum(value_img_grad)
    sum_grid = sum_grad.reshape(seq_count, row_length, width_model)
    caption_input = sum_grid[:, :caption_slots].reshape(seq_count * caption_slots, width_model)
    caption_input = (
        caption_input
        + backward_rows(query_cap_grad, query_back)
        + backward_rows(key_cap_grad, key_back)
        + backward_rows(value_cap_grad, value_back)
    )
    grad_captions = caption_input.reshape(seq_count, caption_slots, width_model)
    region_input = (
        collect_images(sum_grid[:, caption_slots:])
        + backward_rows(query_img_grad, query_back)
        + backward_rows(key_img_grad, key_back)
        + backward_rows(value_img_grad, value_back)
    )
    grad_regions = region_input.reshape(image_count, region_slots, width_model)
    (
        query_weight_part,
        key_weight_part,
        value_weight_part,
        out_weight_part,
        query_bias_part,
        value_bias_part,
        out_bias_part,
        first_gain_part,
        first_shift_part,
        inner_weight_part,
        inner_bias_part,
        outer_weight_part,
        outer_bias_part,
        second_gain_part,
        second_shift_part,
    ) = (
        lax.psum_scatter(query_weight_grad, "fsdp", scatter_dimension=0, tiled=True),
        lax.psum_scatter(key_weight_grad, "fsdp", scatter_dimension=0, tiled=True),
        lax.psum_scatter(value_weight_grad, "fsdp", scatter_dimension=0, tiled=True),
        lax.psum_scatter(out_weight_grad, "fsdp", scatter_dimension=0, tiled=True),
        lax.psum_scatter(query_bias_grad, "fsdp", scatter_dimension=0, tiled=True),
        lax.psum_scatter(value_bias_grad, "fsdp", scatter_dimension=0, tiled=True),
        lax.psum_scatter(out_bias_grad, "fsdp", scatter_dimension=0, tiled=True),
        lax.psum_scatter(first_gain_grad, "fsdp", scatter_dimension=0, tiled=True),
        lax.psum_scatter(first_shift_grad, "fsdp", scatter_dimension=0, tiled=True),
        lax.psum_scatter(inner_weight_grad, "fsdp", scatter_dimension=0, tiled=True),
        lax.psum_scatter(inner_bias_grad, "fsdp", scatter_dimension=0, tiled=True),
        lax.psum_scatter(outer_weight_grad, "fsdp", scatter_dimension=0, tiled=True),
        lax.psum_scatter(outer_bias_grad, "fsdp", scatter_dimension=0, tiled=True),
        lax.psum_scatter(second_gain_grad, "fsdp", scatter_dimension=0, tiled=True),
        lax.psum_scatter(second_shift_grad, "fsdp", scatter_dimension=0, tiled=True),
    )
    (
        query_weight_total,
        key_weight_total,
        value_weight_total,
        out_weight_total,
        query_bias_total,
        value_bias_total,
        out_bias_total,
        first_gain_total,
        first_shift_total,
        inner_weight_total,
        inner_bias_total,
        outer_weight_total,
        outer_bias_total,
        second_gain_total,
        second_shift_total,
    ) = (
        lax.psum(query_weight_part.astype(jnp.bfloat16), "rep").astype(jnp.float32),
        lax.psum(key_weight_part.astype(jnp.bfloat16), "rep").astype(jnp.float32),
        lax.psum(value_weight_part.astype(jnp.bfloat16), "rep").astype(jnp.float32),
        lax.psum(out_weight_part.astype(jnp.bfloat16), "rep").astype(jnp.float32),
        lax.psum(query_bias_part.astype(jnp.bfloat16), "rep").astype(jnp.float32),
        lax.psum(value_bias_part.astype(jnp.bfloat16), "rep").astype(jnp.float32),
        lax.psum(out_bias_part.astype(jnp.bfloat16), "rep").astype(jnp.float32),
        lax.psum(first_gain_part.astype(jnp.bfloat16), "rep").astype(jnp.float32),
        lax.psum(first_shift_part.astype(jnp.bfloat16), "rep").astype(jnp.float32),
        lax.psum(inner_weight_part.astype(jnp.bfloat16), "rep").astype(jnp.float32),
        lax.psum(inner_bias_part.astype(jnp.bfloat16), "rep").astype(jnp.float32),
        lax.psum(outer_weight_part.astype(jnp.bfloat16), "rep").astype(jnp.float32),
        lax.psum(outer_bias_part.astype(jnp.bfloat16), "rep").astype(jnp.float32),
        lax.psum(second_gain_part.astype(jnp.bfloat16), "rep").astype(jnp.float32),
        lax.psum(second_shift_part.astype(jnp.bfloat16), "rep").astype(jnp.float32),
    )
    return (
        out_caption,
        out_region,
        grad_captions,
        grad_regions,
        query_weight_total,
        key_weight_total,
        value_weight_total,
        out_weight_total,
        query_bias_total,
        value_bias_total,
        out_bias_total,
        first_gain_total,
        first_shift_total,
        inner_weight_total,
        inner_bias_total,
        outer_weight_total,
        outer_bias_total,
        second_gain_total,
        second_shift_total,
    )


def solution(mesh):
    return jax.shard_map(
        on_device,
        mesh=mesh,
        in_specs=(
            P(("fsdp", "rep"), None, None),
            P(("fsdp", "rep"), None, None),
            P(("fsdp", "rep")),
            P(("fsdp", "rep")),
            P(("fsdp", "rep")),
            P("fsdp", None),
            P("fsdp", None),
            P("fsdp", None),
            P("fsdp", None),
            P("fsdp"),
            P("fsdp"),
            P("fsdp"),
            P("fsdp"),
            P("fsdp"),
            P("fsdp", None),
            P("fsdp"),
            P("fsdp", None),
            P("fsdp"),
            P("fsdp"),
            P("fsdp"),
            P(("fsdp", "rep"), None, None),
            P(("fsdp", "rep"), None, None),
        ),
        out_specs=(
            P(("fsdp", "rep"), None, None),
            P(("fsdp", "rep"), None, None),
            P(("fsdp", "rep"), None, None),
            P(("fsdp", "rep"), None, None),
            P("fsdp", None),
            P("fsdp", None),
            P("fsdp", None),
            P("fsdp", None),
            P("fsdp"),
            P("fsdp"),
            P("fsdp"),
            P("fsdp"),
            P("fsdp"),
            P("fsdp", None),
            P("fsdp"),
            P("fsdp", None),
            P("fsdp"),
            P("fsdp"),
            P("fsdp"),
        ),
        check_vma=False,
    )
```

profile of v0, /device:TPU:0, one launch (start us, length us, event | category | flops | bytes accessed | tf_op | source)
XLA Modules:
  0.0 1525.7 jit_solution(13391189169871169230)
XLA Ops:
  21.4 79.0 %all-reduce.19 = (bf16[768]{0:T(1024)(128)(2,1)S(1)}, bf16[768]{0:T(1024)(128)(2,1)S(1)}, bf16[768]{0:T(1024)(128)(2,1)S(1)}, bf16[768]{0:T(1024)(128)(2,1)S(1)}...) all-reduce(bf16[768]{0:T(1024)(128)(2,1)S(1)} %dynamic-update-slice, ...), channel_id=1, replica_groups=mesh['fsdp'=16,'rep'=2] {'fsdp'}, use_global_device_ids=true, to_apply=%add | all-reduce | flops 9216 | bytes 36864
  118.5 8.7 all-gather.7.cloned.1.call-done
  133.4 51.3 %all-gather.9.cloned.1.call-done = bf16[768,768]{1,0:T(8,128)(2,1)} async-done(((bf16[48,768]{1,0:T(8,128)(2,1)}), bf16[768,768]{1,0:T(8,128)(2,1)}) %all-gather.9.cloned.1.call-update) | async-done | bytes 1179664 | tf_op jit(solution)/shard_map/all_gather | solution.py:90
  214.2 6.7 copy.157
  225.4 7.3 reshape.296
  239.2 15.9 %fusion.6 = (f32[10,12,256]{2,1,0:T(8,128)S(1)}, f32[10,12,256,256]{2,3,1,0:T(8,128)}) fusion(pred[10,256]{1,0:T(8,128)(4,1)S(1)} %get-tuple-element.155, bf16[10,128,12,64]{1,3,2,0:T(8,128)(2,1)} %bitcast.174, bf16[10,128,12,64]{1,3,2,0:T(8,128)(2,1)} %copy.161, bf16[10,128,12,64]{1,3,2,0:T(8,128)(2,1)S(1)} %bitcast.169, bf16[10,128,12,64]{1,3,2,0:T(8,128)(2,1)} %copy.157), kind=kOutput, calls=%fused_computation.23 | convolution fusion | flops 1045923840 | bytes 39447040 | tf_op jit(solution)/shard_map/sqhe,skhe->shqk/dot_general | solution.py:144
  255.1 15.3 %exponential_reduce_fusion = f32[10,12,256]{2,1,0:T(8,128)S(1)} fusion(f32[10,12,256,256]{2,3,1,0:T(8,128)} %get-tuple-element.159, f32[10,12,256]{2,1,0:T(8,128)S(1)} %get-tuple-element.158, pred[10,256]{1,0:T(8,128)(4,1)S(1)} %get-tuple-element.155), kind=kLoop, calls=%fused_computation.20 | loop fusion | flops 31426560 | bytes 31705600 | tf_op jit(solution)/shard_map/reduce_sum | solution.py:151
  270.5 16.5 %convert_bitcast_fusion = bf16[10,256,12,64]{1,3,2,0:T(8,128)(2,1)} fusion(bf16[10,128,12,64]{1,3,2,0:T(8,128)(2,1)S(1)} %bitcast.172, bf16[10,128,12,64]{1,3,2,0:T(8,128)(2,1)} %copy.153, f32[10,12,256,256]{2,3,1,0:T(8,128)} %get-tuple-element.159, f32[10,12,256]{2,1,0:T(8,128)S(1)} %log_add_fusion, pred[10,256]{1,0:T(8,128)(4,1)S(1)} %get-tuple-element.155), kind=kOutput, calls=%fused_computation.66 | convolution fusion | flops 1047920640 | bytes 39447040 | tf_op jit(solution)/shard_map/shqk,skhe->sqhe/dot_general | solution.py:153
  296.7 7.6 fusion.76
  309.9 13.1 all-gather.15.cloned.1.call-done
  323.1 85.5 %multiply_convert_fusion.1 = (bf16[2560,3072]{1,0:T(8,128)(2,1)}, f32[2560,3072]{1,0:T(8,128)}, f32[2560,3072]{1,0:T(8,128)}) fusion(f32[3072]{0:T(1024)S(1)} %copy-done.47, bf16[768,3072]{1,0:T(8,128)(2,1)} %all-gather.15.cloned.1.call-done, f32[2560,768]{1,0:T(8,128)} %copy-done.3, f32[768]{0:T(1024)S(1)} %copy-done.48, ...), kind=kOutput, calls=%fused_computation.6 | convolution fusion | flops 12608471040 | bytes 91265024 | tf_op jit(solution)/shard_map/dot_general | solution.py:26
  408.6 19.8 %fusion.77 = (f32[2560]{0:T(1024)S(1)}, f32[2560,768]{1,0:T(8,128)S(1)}) fusion(f32[768]{0:T(1024)S(1)} %copy-done.49, bf16[2560,3072]{1,0:T(8,128)(2,1)} %get-tuple-element.145, bf16[3072,768]{1,0:T(8,128)(2,1)} %all-gather.17.cloned.1.call-done, f32[768]{0:T(1024)S(1)} %copy-done.48, f32[768]{0:T(1024)S(1)} %convert_element_type.302, ...), kind=kOutput, calls=%fused_computation.167 | convolution fusion | flops 12093356032 | bytes 36215808 | tf_op jit(solution)/shard_map/dot_general | solution.py:26
  446.8 37.7 %convert_reduce_fusion = (f32[3072]{0:T(1024)}, bf16[2560,3072]{1,0:T(8,128)(2,1)}) fusion(f32[2560,3072]{1,0:T(8,128)} %get-tuple-element.146, bf16[2560,768]{1,0:T(8,128)(2,1)} %get-tuple-element.134, bf16[3072,768]{1,0:T(8,128)(2,1)} %all-gather.17.cloned.1.call-done, f32[2560,3072]{1,0:T(8,128)} %get-tuple-element.162, f32[3072]{0:T(1024)S(1)} %copy-done.47), kind=kOutput, calls=%fused_computation.2 | convolution fusion | flops 12213285888 | bytes 87318528 | tf_op jit(solution)/shard_map/dot_general | solution.py:30
  484.5 25.9 %multiply_reduce_fusion.3 = (f32[768]{0:T(1024)}, f32[2560]{0:T(1024)S(1)}, f32[768]{0:T(1024)}, f32[2560,768]{1,0:T(8,128)}) fusion(f32[2560,768]{1,0:T(8,128)} %copy-done.3, f32[2560]{0:T(1024)S(1)} %fusion.32, f32[2560]{0:T(1024)S(1)} %broadcast_multiply_fusion.3, f32[768]{0:T(1024)S(1)} %convert_element_type.302, ...), kind=kOutput, calls=%fused_computation.33 | convolution fusion | flops 12099251200 | bytes 44090368 | tf_op jit(solution)/shard_map/dot_general | solution.py:30
  510.4 7.3 fusion.70
  527.6 8.5 convolution_convert_fusion
  536.1 12.8 reshape.314
  548.9 11.5 copy.165
  560.4 18.0 %fusion.29 = f32[10,12,64,256]{3,2,1,0:T(8,128)} fusion(bf16[10,256,12,64]{1,3,2,0:T(8,128)(2,1)} %copy.165, f32[10,12,256,256]{2,3,1,0:T(8,128)} %get-tuple-element.159, f32[10,12,256]{2,1,0:T(8,128)S(1)} %copy-done.26, pred[10,256]{1,0:T(8,128)(4,1)S(1)} %copy-done.34), kind=kOutput, calls=%fused_computation.101 | convolution fusion | flops 1038090240 | bytes 43379200 | tf_op jit(solution)/shard_map/shqk,sqhe->skhe/dot_general | solution.py:210
  585.1 6.7 copy.208
  603.7 26.2 %multiply_reduce_fusion = (f32[10,12,256]{2,1,0:T(8,128)S(1)}, f32[10,12,256,256]{2,3,1,0:T(8,128)}) fusion(f32[10,12,256,256]{2,3,1,0:T(8,128)} %get-tuple-element.159, f32[10,12,256]{2,1,0:T(8,128)S(1)} %copy-done.26, pred[10,256]{1,0:T(8,128)(4,1)S(1)} %copy-done.34, bf16[10,256,12,64]{1,3,2,0:T(8,128)(2,1)} %copy.165, ...), kind=kOutput, calls=%fused_computation.4 | convolution fusion | flops 1053788160 | bytes 71027200 | tf_op jit(solution)/shard_map/sqhe,skhe->shqk/dot_general | solution.py:207
  629.9 28.0 %multiply_convert_fusion = bf16[10,12,256,256]{2,3,1,0:T(8,128)(2,1)} fusion(f32[10,12,256,256]{2,3,1,0:T(8,128)} %get-tuple-element.167, f32[10,12,256,256]{2,3,1,0:T(8,128)} %get-tuple-element.159, f32[10,12,256]{2,1,0:T(8,128)S(1)} %get-tuple-element.166, f32[10,12,256]{2,1,0:T(8,128)S(1)} %copy-done.26, pred[10,256]{1,0:T(8,128)(4,1)S(1)} %copy-done.34), kind=kLoop, calls=%fused_computation.3 | loop fusion | flops 47185920 | bytes 78891520 | tf_op jit(solution)/shard_map/convert_element_type | solution.py:217
  657.9 11.6 broadcast_multiply_fusion
  692.2 9.6 broadcast_multiply_fusion.1
  724.0 21.1 %fusion.66 = f32[768,3072]{1,0:T(8,128)} fusion(bf16[2560,3072]{1,0:T(8,128)(2,1)} %get-tuple-element.173, f32[2560,768]{1,0:T(8,128)} %copy-done.3, f32[768]{0:T(1024)} %convert_element_type.303, f32[768]{0:T(1024)S(1)} %copy-done.46, f32[2560]{0:T(1024)} %copy-done.35, f32[2560]{0:T(1024)S(1)} %broadcast_multiply_fusion.3), kind=kOutput, calls=%fused_computation.159 | convolution fusion | flops 12089425920 | bytes 33056768 | tf_op jit(solution)/shard_map/dot_general | solution.py:36
  745.2 18.6 %fusion.84 = f32[3072,768]{1,0:T(8,128)} fusion(bf16[2560,3072]{1,0:T(8,128)(2,1)} %get-tuple-element.145, bf16[2560,768]{1,0:T(8,128)(2,1)} %get-tuple-element.134), kind=kOutput, calls=%fused_computation.174 | convolution fusion | flops 12079595520 | bytes 29097984 | tf_op jit(solution)/shard_map/dot_general | solution.py:36
  809.1 113.7 %reduce-scatter.21.cloned.1.call-done = f32[48,768]{1,0:T(8,128)} async-done(((f32[768,768]{1,0:T(8,128)}), f32[48,768]{1,0:T(8,128)}) %reduce-scatter.21.cloned.1.call-update) | async-done | bytes 147472
  924.5 131.6 %reduce-scatter.19.cloned.1.call-done = f32[48,768]{1,0:T(8,128)} async-done(((f32[768,768]{1,0:T(8,128)}), f32[48,768]{1,0:T(8,128)}) %reduce-scatter.19.cloned.1.call-update) | async-done | bytes 147472
  1057.9 174.1 %reduce-scatter.15.cloned.1.call-done = f32[48,3072]{1,0:T(8,128)} async-done(((f32[768,3072]{1,0:T(8,128)}), f32[48,3072]{1,0:T(8,128)}) %reduce-scatter.15.cloned.1.call-update) | async-done | bytes 589840 | tf_op jit(solution)/shard_map/reduce_scatter | solution.py:289
  1233.8 174.7 %reduce-scatter.17.cloned.1.call-done = f32[192,768]{1,0:T(8,128)} async-done(((f32[3072,768]{1,0:T(8,128)}), f32[192,768]{1,0:T(8,128)}) %reduce-scatter.17.cloned.1.call-update) | async-done | bytes 589840 | tf_op jit(solution)/shard_map/reduce_scatter | solution.py:291
  1416.1 75.9 %all-reduce.18 = (bf16[768]{0:T(1024)(128)(2,1)S(1)}, bf16[768]{0:T(1024)(128)(2,1)S(1)}, bf16[768]{0:T(1024)(128)(2,1)S(1)}, bf16[768]{0:T(1024)(128)(2,1)S(1)}...) all-reduce(f32[768]{0:T(1024)S(1)} %add.247, ...), channel_id=6, replica_groups=mesh['fsdp'=16,'rep'=2] {'fsdp'}, use_global_device_ids=true, to_apply=%region_22.23.clone | all-reduce | flops 9216 | bytes 55296
  1499.7 8.7 fusion.14
  (276 shorter events, 258.9 us)
Async XLA Ops:
  7.2 100.1 %copy-start = (bf16[2,128,768]{2,1,0:T(8,128)(2,1)S(1)}, bf16[2,128,768]{2,1,0:T(8,128)(2,1)}, u32[]{:S(2)}) copy-start(bf16[2,128,768]{2,1,0:T(8,128)(2,1)} %param.23) | copy-start | bytes 1179652
  7.2 102.7 %copy-start.23 = (bf16[10,128,768]{2,1,0:T(8,128)(2,1)S(1)}, bf16[10,128,768]{2,1,0:T(8,128)(2,1)}, u32[]{:S(2)}) copy-start(bf16[10,128,768]{2,1,0:T(8,128)(2,1)} %param.22) | copy-start | bytes 5898244
  7.2 104.9 %all-gather.11.cloned.1.call-start = ((), (), s32[]{:S(2)}) async-start(), calls=%async_computation.8 | async-start | bytes 1253376 | tf_op jit(solution)/shard_map/all_gather | solution.py:91
  8.0 119.2 %all-gather.7.cloned.1.call-start = ((), (), s32[]{:S(2)}) async-start(), calls=%async_computation.6 | async-start | bytes 1253376 | tf_op jit(solution)/shard_map/all_gather | solution.py:92
  8.7 175.9 %all-gather.9.cloned.1.call-start = ((), (), s32[]{:S(2)}) async-start(), calls=%async_computation.7 | async-start | bytes 1253376 | tf_op jit(solution)/shard_map/all_gather | solution.py:90
  9.4 287.3 %all-gather.13.cloned.1.call-start = ((), (), s32[]{:S(2)}) async-start(), calls=%async_computation.9 | async-start | bytes 1253376 | tf_op jit(solution)/shard_map/all_gather | solution.py:93
  10.0 313.0 %all-gather.15.cloned.1.call-start = ((), (), s32[]{:S(2)}) async-start(), calls=%async_computation.10 | async-start | bytes 5013504 | tf_op jit(solution)/shard_map/all_gather | solution.py:170
  10.6 398.0 %all-gather.17.cloned.1.call-start = ((), (), s32[]{:S(2)}) async-start(), calls=%async_computation.11 | async-start | bytes 5013504 | tf_op jit(solution)/shard_map/all_gather | solution.py:172
  11.2 794.6 %reduce-scatter.13.cloned.1.call-start = ((), (), s32[]{:S(2)}) async-start(), calls=%async_computation.12 | async-start | bytes 2506752 | tf_op jit(solution)/shard_map/reduce_scatter | solution.py:283
  101.0 409.3 %copy-start.45 = (f32[768]{0:T(1024)}, f32[768]{0:T(1024)S(1)}, u32[]{:S(2)}) copy-start(f32[768]{0:T(1024)S(1)} %convert_element_type.302) | copy-start | bytes 9220
  106.7 163.9 %copy-start.33 = (pred[10,256]{1,0:T(8,128)(4,1)}, pred[10,256]{1,0:T(8,128)(4,1)S(1)}, u32[]{:S(2)}) copy-start(pred[10,256]{1,0:T(8,128)(4,1)S(1)} %get-tuple-element.155) | copy-start | bytes 7684
  109.9 17.3 %copy-start.51 = (f32[768]{0:T(1024)S(1)}, f32[768]{0:T(1024)}, u32[]{:S(2)}) copy-start(f32[768]{0:T(1024)} %convert_element_type.287) | copy-start | bytes 9220
  255.1 15.4 %copy-start.12 = (bf16[10,128,768]{1,2,0:T(8,128)(2,1)S(1)}, bf16[10,128,768]{1,2,0:T(8,128)(2,1)}, u32[]{:S(2)}) copy-start(bf16[10,128,768]{1,2,0:T(8,128)(2,1)} %copy.152) | copy-start | bytes 5898244
  270.5 16.5 %copy-start.25 = (f32[10,12,256]{2,1,0:T(8,128)}, f32[10,12,256]{2,1,0:T(8,128)S(1)}, u32[]{:S(2)}) copy-start(f32[10,12,256]{2,1,0:T(8,128)S(1)} %log_add_fusion) | copy-start | bytes 368644
  304.4 18.6 %copy-start.47 = (f32[3072]{0:T(1024)S(1)}, f32[3072]{0:T(1024)}, u32[]{:S(2)}) copy-start(f32[3072]{0:T(1024)} %convert_element_type.305) | copy-start | bytes 36868
  304.4 18.6 %copy-start.48 = (f32[768]{0:T(1024)S(1)}, f32[768]{0:T(1024)}, u32[]{:S(2)}) copy-start(f32[768]{0:T(1024)} %convert_element_type.303) | copy-start | bytes 9220
  309.9 200.4 %copy-start.35 = (f32[2560]{0:T(1024)}, f32[2560]{0:T(1024)S(1)}, u32[]{:S(2)}) copy-start(f32[2560]{0:T(1024)S(1)} %fusion.32) | copy-start | bytes 30724
  323.1 85.5 %copy-start.49 = (f32[768]{0:T(1024)S(1)}, f32[768]{0:T(1024)}, u32[]{:S(2)}) copy-start(f32[768]{0:T(1024)} %convert_element_type.307) | copy-start | bytes 9220
  484.5 25.9 %copy-start.32 = (f32[2560]{0:T(1024)S(1)}, f32[2560]{0:T(1024)}, u32[]{:S(2)}) copy-start(f32[2560]{0:T(1024)} %copy-done.31) | copy-start | bytes 30724
  527.4 280.0 %reduce-scatter.23.cloned.1.call-start = ((), (), s32[]{:S(2)}) async-start(), calls=%async_computation.17 | async-start | bytes 2506752
  629.9 292.9 %reduce-scatter.21.cloned.1.call-start = ((), (), s32[]{:S(2)}) async-start(), calls=%async_computation.16 | async-start | bytes 2506752
  629.9 28.0 %copy-start.11 = (bf16[10,128,768]{1,2,0:T(8,128)(2,1)S(1)}, bf16[10,128,768]{1,2,0:T(8,128)(2,1)}, u32[]{:S(2)}) copy-start(bf16[10,128,768]{1,2,0:T(8,128)(2,1)} %copy.156) | copy-start | bytes 5898244
  691.8 364.3 %reduce-scatter.19.cloned.1.call-start = ((), (), s32[]{:S(2)}) async-start(), calls=%async_computation.15 | async-start | bytes 2506752
  723.8 508.2 %reduce-scatter.15.cloned.1.call-start = ((), (), s32[]{:S(2)}) async-start(), calls=%async_computation.13 | async-start | bytes 10027008 | tf_op jit(solution)/shard_map/reduce_scatter | solution.py:289
  745.2 663.3 %reduce-scatter.17.cloned.1.call-start = ((), (), s32[]{:S(2)}) async-start(), calls=%async_computation.14 | async-start | bytes 10027008 | tf_op jit(solution)/shard_map/reduce_scatter | solution.py:291
  763.9 744.6 %all-reduce.24.cloned.1.call-start = ((), (), s32[]{:S(2)}) async-start(), calls=%async_computation.18 | async-start | bytes 2506752 | tf_op jit(solution)/shard_map/psum | solution.py:313
  802.0 608.3 %copy-start.15 = (bf16[768,768]{1,0:T(8,128)(2,1)S(1)}, bf16[768,768]{1,0:T(8,128)(2,1)}, u32[]{:S(2)}) copy-start(bf16[768,768]{1,0:T(8,128)(2,1)} %all-gather.7.cloned.1.call-done) | copy-start | bytes 3538948
  802.0 610.9 %copy-start.9 = (bf16[10,128,768]{1,2,0:T(8,128)(2,1)S(1)}, bf16[10,128,768]{1,2,0:T(8,128)(2,1)}, u32[]{:S(2)}) copy-start(bf16[10,128,768]{1,2,0:T(8,128)(2,1)} %copy-done.8) | copy-start | bytes 5898244
  805.7 609.6 %copy-start.41 = (f32[768]{0:T(1024)S(1)}, f32[768]{0:T(1024)}, u32[]{:S(2)}) copy-start(f32[768]{0:T(1024)} %get-tuple-element.137) | copy-start | bytes 9220
  805.7 609.6 %copy-start.42 = (f32[768]{0:T(1024)S(1)}, f32[768]{0:T(1024)}, u32[]{:S(2)}) copy-start(f32[768]{0:T(1024)} %get-tuple-element.170) | copy-start | bytes 9220
  805.7 609.6 %copy-start.43 = (f32[768]{0:T(1024)S(1)}, f32[768]{0:T(1024)}, u32[]{:S(2)}) copy-start(f32[768]{0:T(1024)} %get-tuple-element.139) | copy-start | bytes 9220
  805.7 610.3 %copy-start.40 = (f32[768]{0:T(1024)S(1)}, f32[768]{0:T(1024)}, u32[]{:S(2)}) copy-start(f32[768]{0:T(1024)} %get-tuple-element.97) | copy-start | bytes 9220
  (35 other events, 221.6 us)
Sparse Core Ops, SparseCore 0:
  10.8 58.8 all-gather.10
  72.5 54.6 all-gather.6
  130.0 54.6 all-gather.8
  187.3 54.6 all-gather.12
  244.6 78.4 all-gather.14
  325.7 78.3 all-gather.16
  527.5 128.2 reduce-scatter.12
  660.7 128.5 reduce-scatter.22
  794.2 128.5 reduce-scatter.20
  927.5 128.5 reduce-scatter.18
  1061.8 170.1 reduce-scatter.14
  1237.5 170.8 reduce-scatter.16
  1412.4 19.3 all-reduce.23
where the time goes:
time: 1540 us; the launch traced here: 1530 us
  waiting for transfers between devices  671 us (44%)
  matrix products  408 us (26%)
  local copies, waits for them, and re-layouts  164 us (11%)
  blocking collectives  157 us (10%)
  other arithmetic  106 us (7%)
  between operations  17.9 us (1%)
    unnamed x16, waiting for transfers between devices  249 us
    reduce_scatter x1, waiting for transfers between devices, on_device(): lax.psum_scatter(outer_weight_grad, 'fsdp', scatter_dimension=0, tiled=True)  175 us
    reduce_scatter x1, waiting for transfers between devices, on_device(): lax.psum_scatter(inner_weight_grad, 'fsdp', scatter_dimension=0, tiled=True)  174 us
    unnamed x2, blocking collectives  155 us
    dot_general x9, matrix products, forward_rows(): return jnp.dot(row_block, weight, preferred_element_type=jnp.float32)  130 us
    dot_general x9, matrix products, backward_rows(): lax.dot_general(gradient, weight, (((1,), (1,)), ((), ())), preferred_ele...  95.9 us
    unnamed x149, local copies, waits for them, and re-layouts  60.3 us
    dot_general x9, matrix products, weight_grad(): lax.dot_general(row_block, gradient, (((0,), (0,)), ((), ())), preferred_...  56.4 us
  transfers between devices with their start and end apart: 13, of which 7 were waited for; matrix products, arithmetic and copies ran while one was open for 36% of the time, Pallas kernels for 0%

commit v1 on v0

--- a/solution.py
+++ b/solution.py
@@ -1,6 +1,10 @@
+import functools
+
 import jax
 import jax.numpy as jnp
 from jax import lax
+from jax.experimental import pallas as pl
+from jax.experimental.pallas import tpu as pltpu
 from jax.sharding import PartitionSpec as P
 
 HEADS = 12
@@ -42,7 +46,503 @@
     return jnp.sum(gradient.astype(jnp.float32), axis=0)
 
 
+MESH = pl.DeviceIdType.MESH
+PLANES = 4
+COLUMN_SPLIT, ROW_SPLIT = 0, 1
+
+
+def place_of(index, half, step, first, second):
+    across = first * (1 - half) + second * half
+    down = second * (1 - half) + first * half
+    plane = lax.rem(index // 4 + step, PLANES)
+    row = lax.rem(lax.rem(index // 2, 2) + down, 2)
+    column = lax.rem(lax.rem(index, 2) + across, 2)
+    return plane * 4 + row * 2 + column
+
+
+def part_of(ref, split, owner, half, count, align):
+    rows, columns = ref.shape[0] // count, ref.shape[1]
+    if split == COLUMN_SPLIT:
+        width = columns // 2
+        return ref.at[
+            pl.ds(pl.multiple_of(owner * rows, align), rows),
+            pl.ds(pl.multiple_of(half * width, 128), width),
+        ]
+    height = rows // 2
+    return ref.at[pl.ds(pl.multiple_of(owner * rows + half * height, align), height)]
+
+
+def greet(index, half):
+    barrier = pltpu.get_barrier_semaphore()
+    peers = [(place_of(index, half, step, 0, 0), half) for step in (1, 2, 3)]
+    peers += [(place_of(index, half, 0, 1, 0), half), (place_of(index, half, 0, 0, 1), half)]
+    peers += [(index, 1 - half)]
+    for peer in peers:
+        pl.semaphore_signal(barrier, inc=1, device_id=peer, device_id_type=MESH)
+    pl.semaphore_wait(barrier, len(peers))
+
+
+def gather_kernel(splits, aligns, *refs):
+    count = len(splits)
+    shards, wholes = refs[:count], refs[count : 2 * count]
+    (own_sem, z_send, z_recv, a_send, a_recv, b_send, b_recv, s_send, s_recv) = refs[2 * count :]
+    index, half = lax.axis_index("fsdp"), lax.axis_index("rep")
+    owners = wholes[0].shape[0] // shards[0].shape[0]
+
+    def owner_of(step, first, second):
+        return place_of(index, half, step, first, second)
+
+    def piece(tensor, step, first, second):
+        owner = owner_of(step, first, second)
+        return part_of(wholes[tensor], splits[tensor], owner, half, owners, aligns[tensor])
+
+    def copy_piece(tensor, source, step, first, second, send, recv, peer):
+        return pltpu.make_async_remote_copy(
+            src_ref=source,
+            dst_ref=piece(tensor, step, first, second),
+            send_sem=send,
+            recv_sem=recv,
+            device_id=peer,
+            device_id_type=MESH,
+        )
+
+    peer_a = (owner_of(0, 1, 0), half)
+    peer_b = (owner_of(0, 0, 1), half)
+    sibling = (index, 1 - half)
+
+    def to_z(tensor, source, hop):
+        peer = (owner_of(hop, 0, 0), half)
+        slot = PLANES - hop - 1
+        return copy_piece(
+            tensor, source, 0, 0, 0, z_send.at[tensor, hop - 1], z_recv.at[tensor, slot], peer
+        )
+
+    def to_a(tensor, source, step):
+        return copy_piece(
+            tensor, source, step, 0, 0, a_send.at[tensor, step], a_recv.at[tensor, step], peer_a
+        )
+
+    def to_b(tensor, source, step, first):
+        slot = step * 2 + first
+        return copy_piece(
+            tensor, source, step, first, 0, b_send.at[tensor, slot], b_recv.at[tensor, slot], peer_b
+        )
+
+    def to_sibling(tensor, source, step, first, second):
+        slot = step * 4 + first * 2 + second - 1
+        return copy_piece(
+            tensor,
+            source,
+            step,
+            first,
+            second,
+            s_send.at[tensor, slot],
+            s_recv.at[tensor, slot],
+            sibling,
+        )
+
+    greet(index, half)
+    started = []
+    local = []
+    for tensor in range(count):
+        shard = shards[tensor]
+        rows = shard.shape[0]
+        source = part_of(shard, splits[tensor], 0, half, 1, aligns[tensor])
+        sends = [to_z(tensor, source, hop) for hop in (1, 2, 3)]
+        sends += [to_a(tensor, source, 0), to_b(tensor, source, 0, 0)]
+        for copy in sends:
+            copy.start()
+        started += sends
+        here = pltpu.make_async_copy(
+            shard,
+            wholes[tensor].at[pl.ds(pl.multiple_of(index * rows, aligns[tensor]), rows)],
+            own_sem.at[tensor],
+        )
+        here.start()
+        local.append(here)
+    for tensor in range(count):
+        for step in (1, 2, 3):
+            source = piece(tensor, step, 0, 0)
+            copy_piece(
+                tensor,
+                source,
+                step,
+                0,
+                0,
+                z_send.at[tensor, step - 1],
+                z_recv.at[tensor, step - 1],
+                sibling,
+            ).wait_recv()
+            sends = [
+                to_b(tensor, source, step, 0),
+                to_a(tensor, source, step),
+                to_sibling(tensor, source, step, 0, 0),
+            ]
+            for copy in sends:
+                copy.start()
+            started += sends
+    for tensor in range(count):
+        for step in range(PLANES):
+            source = piece(tensor, step, 1, 0)
+            copy_piece(
+                tensor,
+                source,
+                step,
+                1,
+                0,
+                a_send.at[tensor, step],
+                a_recv.at[tensor, step],
+                peer_a,
+            ).wait_recv()
+            sends = [to_b(tensor, source, step, 1), to_sibling(tensor, source, step, 1, 0)]
+            for copy in sends:
+                copy.start()
+            started += sends
+    for tensor in range(count):
+        for step in range(PLANES):
+            for first in (0, 1):
+                source = piece(tensor, step, first, 1)
+                slot = step * 2 + first
+                copy_piece(
+                    tensor,
+                    source,
+                    step,
+                    first,
+                    1,
+                    b_send.at[tensor, slot],
+                    b_recv.at[tensor, slot],
+                    peer_b,
+                ).wait_recv()
+                copy = to_sibling(tensor, source, step, first, 1)
+                copy.start()
+                started.append(copy)
+    for tensor in range(count):
+        local[tensor].wait()
+        for step in range(PLANES):
+            for first in (0, 1):
+                for second in (0, 1):
+                    if step + first + second == 0:
+                        continue
+                    slot = step * 4 + first * 2 + second - 1
+                    owner = place_of(index, 1 - half, step, first, second)
+                    there = part_of(
+                        wholes[tensor], splits[tensor], owner, 1 - half, owners, aligns[tensor]
+                    )
+                    pltpu.make_async_remote_copy(
+                        src_ref=there,
+                        dst_ref=there,
+                        send_sem=s_send.at[tensor, slot],
+                        recv_sem=s_recv.at[tensor, slot],
+                        device_id=sibling,
+                        device_id_type=MESH,
+                    ).wait_recv()
+    for copy in started:
+        copy.wait_send()
+
+
+def gather_all(shards, splits, owners, collective_id):
+    count = len(shards)
+    aligns = [16 if shard.dtype == jnp.bfloat16 else 8 for shard in shards]
+    dma = pltpu.SemaphoreType.DMA
+    return pl.pallas_call(
+        functools.partial(gather_kernel, splits, aligns),
+        out_shape=[
+            jax.ShapeDtypeStruct((owners * shard.shape[0], shard.shape[1]), shard.dtype)
+            for shard in shards
+        ],
+        in_specs=[pl.BlockSpec(memory_space=pltpu.VMEM)] * count,
+        out_specs=[pl.BlockSpec(memory_space=pl.ANY)] * count,
+        scratch_shapes=[
+            dma((count,)),
+            dma((count, 3)),
+            dma((count, 3)),
+            dma((count, 4)),
+            dma((count, 4)),
+            dma((count, 8)),
+            dma((count, 8)),
+            dma((count, 15)),
+            dma((count, 15)),
+        ],
+        compiler_params=pltpu.CompilerParams(collective_id=collective_id, has_side_effects=True),
+        name="gather_rows",
+    )(*shards)
+
+
+def reduce_kernel(splits, aligns, owners, *refs):
+    count = len(splits)
+    partials, totals = refs[:count], refs[count : 2 * count]
+    mine = refs[2 * count : 3 * count]
+    core_in = refs[3 * count : 4 * count]
+    b_in = refs[4 * count : 5 * count]
+    a_in = refs[5 * count : 6 * count]
+    z_in = refs[6 * count : 7 * count]
+    (load_sem, c_send, c_recv, b_send, b_recv, a_send, a_recv, z_send, z_recv, o_send, o_recv) = (
+        refs[7 * count :]
+    )
+    index, half = lax.axis_index("fsdp"), lax.axis_index("rep")
+    sibling = (index, 1 - half)
+    peer_a = (place_of(index, half, 0, 1, 0), half)
+    peer_b = (place_of(index, half, 0, 0, 1), half)
+
+    def slot_of(step, first, second):
+        return second * 8 + first * 4 + step
+
+    def load(tensor, step, first, second):
+        owner = place_of(index, half, step, first, second)
+        slot = slot_of(step, first, second)
+        return pltpu.make_async_copy(
+            part_of(partials[tensor], splits[tensor], owner, half, owners, aligns[tensor]),
+            mine[tensor].at[slot],
+            load_sem.at[tensor, slot],
+        )
+
+    def to_core(tensor, step, first, second):
+        owner = place_of(index, 1 - half, step, first, second)
+        slot = slot_of(step, first, second)
+        return pltpu.make_async_remote_copy(
+            src_ref=part_of(
+                partials[tensor], splits[tensor], owner, 1 - half, owners, aligns[tensor]
+            ),
+            dst_ref=core_in[tensor].at[slot],
+            send_sem=c_send.at[tensor, slot],
+            recv_sem=c_recv.at[tensor, slot],
+            device_id=sibling,
+            device_id_type=MESH,
+        )
+
+    def to_b(tensor, step, first):
+        slot = first * 4 + step
+        return pltpu.make_async_remote_copy(
+            src_ref=mine[tensor].at[8 + slot],
+            dst_ref=b_in[tensor].at[slot],
+            send_sem=b_send.at[tensor, slot],
+            recv_sem=b_recv.at[tensor, slot],
+            device_id=peer_b,
+            device_id_type=MESH,
+        )
+
+    def to_a(tensor, step):
+        return pltpu.make_async_remote_copy(
+            src_ref=mine[tensor].at[4 + step],
+            dst_ref=a_in[tensor].at[step],
+            send_sem=a_send.at[tensor, step],
+            recv_sem=a_recv.at[tensor, step],
+            device_id=peer_a,
+            device_id_type=MESH,
+        )
+
+    def to_z(tensor, hop):
+        return pltpu.make_async_remote_copy(
+            src_ref=mine[tensor].at[hop],
+            dst_ref=z_in[tensor].at[PLANES - hop - 1],
+            send_sem=z_send.at[tensor, hop - 1],
+            recv_sem=z_recv.at[tensor, PLANES - hop - 1],
+            device_id=(place_of(index, half, hop, 0, 0), half),
+            device_id_type=MESH,
+        )
+
+    def wide(ref):
+        return ref[...].astype(jnp.float32)
+
+    def output_part(tensor):
+        return part_of(totals[tensor], splits[tensor], 0, half, 1, 8)
+
+    def to_output(tensor):
+        return pltpu.make_async_remote_copy(
+            src_ref=output_part(tensor),
+            dst_ref=output_part(tensor),
+            send_sem=o_send.at[tensor],
+            recv_sem=o_recv.at[tensor],
+            device_id=sibling,
+            device_id_type=MESH,
+        )
+
+    greet(index, half)
+
+    order = [(step, first, 1) for first in (1, 0) for step in (1, 2, 3, 0)]
+    order += [(step, 1, 0) for step in (1, 2, 3, 0)] + [(step, 0, 0) for step in (1, 2, 3, 0)]
+    for tensor in range(count):
+        for step, first, second in order:
+            to_core(tensor, step, first, second).start()
+            load(tensor, step, first, second).start()
+
+    for tensor in range(count):
+
+        def b_step(turn, carry, tensor=tensor):
+            step, first = lax.rem(turn + 1, PLANES), 1 - turn // PLANES
+            load(tensor, step, first, 1).wait()
+            to_core(tensor, step, first, 1).wait_recv()
+            slot = slot_of(step, first, 1)
+            total = wide(mine[tensor].at[slot]) + wide(core_in[tensor].at[slot])
+            mine[tensor].at[slot][...] = total.astype(mine[tensor].dtype)
+            to_b(tensor, step, first).start()
+            return carry
+
+        lax.fori_loop(0, 2 * PLANES, b_step, 0)
+    for tensor in range(count):
+
+        def a_step(turn, carry, tensor=tensor):
+            step = lax.rem(turn + 1, PLANES)
+            load(tensor, step, 1, 0).wait()
+            to_core(tensor, step, 1, 0).wait_recv()
+            to_b(tensor, step, 1).wait_recv()
+            slot = slot_of(step, 1, 0)
+            total = wide(mine[tensor].at[slot]) + wide(core_in[tensor].at[slot])
+            total += wide(b_in[tensor].at[slot])
+            mine[tensor].at[slot][...] = total.astype(mine[tensor].dtype)
+            to_a(tensor, step).start()
+            return carry
+
+        lax.fori_loop(0, PLANES, a_step, 0)
+    for tensor in range(count):
+
+        def total_of(step, tensor=tensor):
+            load(tensor, step, 0, 0).wait()
+            to_core(tensor, step, 0, 0).wait_recv()
+            to_b(tensor, step, 0).wait_recv()
+            to_a(tensor, step).wait_recv()
+            total = wide(mine[tensor].at[step]) + wide(core_in[tensor].at[step])
+            return total + wide(b_in[tensor].at[step]) + wide(a_in[tensor].at[step])
+
+        for hop in (1, 2, 3):
+            mine[tensor].at[hop][...] = total_of(hop).astype(mine[tensor].dtype)
+            to_z(tensor, hop).start()
+        mine_total = total_of(0)
+        output_part(tensor)[...] = mine_total
+    for tensor in range(count):
+        out = output_part(tensor)
+        total = out[...]
+        for hop in (1, 2, 3):
+            slot = PLANES - hop - 1
+            pltpu.make_async_remote_copy(
+                src_ref=mine[tensor].at[hop],
+                dst_ref=z_in[tensor].at[slot],
+                send_sem=z_send.at[tensor, hop - 1],
+                recv_sem=z_recv.at[tensor, slot],
+                device_id=sibling,
+                device_id_type=MESH,
+            ).wait_recv()
+            total += wide(z_in[tensor].at[slot])
+        out[...] = total
+        to_output(tensor).start()
+    for tensor in range(count):
+        pltpu.make_async_remote_copy(
+            src_ref=part_of(totals[tensor], splits[tensor], 0, 1 - half, 1, 8),
+            dst_ref=part_of(totals[tensor], splits[tensor], 0, 1 - half, 1, 8),
+            send_sem=o_send.at[tensor],
+            recv_sem=o_recv.at[tensor],
+            device_id=sibling,
+            device_id_type=MESH,
+        ).wait_recv()
+        to_output(tensor).wait_send()
+        for step, first, second in order:
+            to_core(tensor, step, first, second).wait_send()
+            if second == 1:
+                to_b(tensor, step, first).wait_send()
+            elif first == 1:
+                to_a(tensor, step).wait_send()
+            elif step > 0:
+                to_z(tensor, step).wait_send()
+
+
+def reduce_all(partials, splits, owners, collective_id):
+    count = len(partials)
+    aligns = [16 if part.dtype == jnp.bfloat16 else 8 for part in partials]
+    dma = pltpu.SemaphoreType.DMA
+
+    def pieces(slots):
+        shapes = []
+        for part, split in zip(partials, splits):
+            rows, columns = part.shape[0] // owners, part.shape[1]
+            shape = (rows, columns // 2) if split == COLUMN_SPLIT else (rows // 2, columns)
+            shapes.append(pltpu.VMEM((slots, *shape), part.dtype))
+        return shapes
+
+    return pl.pallas_call(
+        functools.partial(reduce_kernel, splits, aligns, owners),
+        out_shape=[
+            jax.ShapeDtypeStruct((part.shape[0] // owners, part.shape[1]), jnp.float32)
+            for part in partials
+        ],
+        in_specs=[pl.BlockSpec(memory_space=pl.ANY)] * count,
+        out_specs=[pl.BlockSpec(memory_space=pltpu.VMEM)] * count,
+        scratch_shapes=[
+            *pieces(16),
+            *pieces(16),
+            *pieces(8),
+            *pieces(4),
+            *pieces(3),
+            dma((count, 16)),
+            dma((count, 16)),
+            dma((count, 16)),
+            dma((count, 8)),
+            dma((count, 8)),
+            dma((count, 4)),
+            dma((count, 4)),
+            dma((count, 3)),
+            dma((count, 3)),
+            dma((count,)),
+            dma((count,)),
+        ],
+        compiler_params=pltpu.CompilerParams(
+            collective_id=collective_id, has_side_effects=True, vmem_limit_bytes=48 * 1024 * 1024
+        ),
+        name="reduce_rows",
+    )(*partials)
+
+
+OWNERS = 16
+VECTOR_ROWS = 16
+WEIGHT_SPLITS = (COLUMN_SPLIT, COLUMN_SPLIT, ROW_SPLIT, ROW_SPLIT)
+
+
+def pack_vectors(parts, owners):
+    grid = jnp.concatenate([p.astype(jnp.float32).reshape(owners, -1) for p in parts], axis=1)
+    grid = jnp.pad(grid, ((0, 0), (0, VECTOR_ROWS * 128 - grid.shape[1])))
+    return grid.reshape(owners * VECTOR_ROWS, 128)
+
+
+def unpack_vectors(rows, owners, sizes):
+    grid = rows.reshape(owners, VECTOR_ROWS * 128)
+    vectors, start = [], 0
+    for size in sizes:
+        vectors.append(grid[:, start : start + size].reshape(owners * size))
+        start += size
+    return vectors
+
+
+def gather_weights(matrices, vectors, use_kernels):
+    if not use_kernels:
+        whole = [lax.all_gather(m, "fsdp", axis=0, tiled=True) for m in (*matrices, *vectors)]
+        return whole[: len(matrices)], whole[len(matrices) :]
+    square = jnp.concatenate(matrices[:4], axis=1)
+    packed = pack_vectors(vectors, 1)
+    square, inner, outer, packed = gather_all(
+        (square, matrices[4], matrices[5], packed), WEIGHT_SPLITS, OWNERS, 1
+    )
+    whole_vectors = unpack_vectors(packed, OWNERS, [v.shape[0] for v in vectors])
+    return [*jnp.split(square, 4, axis=1), inner, outer], whole_vectors
+
+
+def reduce_weights(matrices, vectors, use_kernels):
+    if not use_kernels:
+        totals = []
+        for part in (*matrices, *vectors):
+            share = lax.psum_scatter(part, "fsdp", scatter_dimension=0, tiled=True)
+            totals.append(lax.psum(share.astype(jnp.bfloat16), "rep").astype(jnp.float32))
+        return totals[: len(matrices)], totals[len(matrices) :]
+    low = [m.astype(jnp.bfloat16) for m in matrices]
+    square = jnp.concatenate(low[:4], axis=1)
+    packed = pack_vectors(vectors, OWNERS)
+    square, inner, outer, packed = reduce_all(
+        (square, low[4], low[5], packed), WEIGHT_SPLITS, OWNERS, 2
+    )
+    sizes = [v.shape[0] // OWNERS for v in vectors]
+    return [*jnp.split(square, 4, axis=1), inner, outer], unpack_vectors(packed, 1, sizes)
+
+
 def on_device(
+    use_kernels,
     captions,
     regions,
     caption_lengths,
@@ -76,27 +576,32 @@
     head_size = width_model // head_count
     scaling = head_size ** (-0.5)
     all_rows = seq_count * row_length
+    (query_all, key_all, value_all, out_all, inner_all, outer_all), whole_vectors = gather_weights(
+        (query_weight, key_weight, value_weight, out_weight, inner_weight, outer_weight),
+        (
+            query_bias,
+            value_bias,
+            out_bias,
+            first_gain,
+            first_shift,
+            inner_bias,
+            outer_bias,
+            second_gain,
+            second_shift,
+        ),
+        use_kernels,
+    )
     (
-        query_all,
-        key_all,
-        value_all,
-        out_all,
         query_offset,
         value_offset,
         out_offset,
         gain_first,
         shift_first,
-    ) = (
-        lax.all_gather(query_weight, "fsdp", axis=0, tiled=True),
-        lax.all_gather(key_weight, "fsdp", axis=0, tiled=True),
-        lax.all_gather(value_weight, "fsdp", axis=0, tiled=True),
-        lax.all_gather(out_weight, "fsdp", axis=0, tiled=True),
-        lax.all_gather(query_bias, "fsdp", axis=0, tiled=True),
-        lax.all_gather(value_bias, "fsdp", axis=0, tiled=True),
-        lax.all_gather(out_bias, "fsdp", axis=0, tiled=True),
-        lax.all_gather(first_gain, "fsdp", axis=0, tiled=True),
-        lax.all_gather(first_shift, "fsdp", axis=0, tiled=True),
-    )
+        inner_offset,
+        outer_offset,
+        gain_second,
+        shift_second,
+    ) = whole_vectors
     image_match = group_ids[:, None] == jnp.arange(image_count, dtype=jnp.int32)[None, :]
     match_low = image_match.astype(jnp.bfloat16)
     match_float = image_match.astype(jnp.float32)
@@ -166,14 +671,6 @@
         normalize, first_sum, gain_first.astype(jnp.float32), shift_first.astype(jnp.float32)
     )
     first_low = first_out.astype(jnp.bfloat16)
-    inner_all, inner_offset, outer_all, outer_offset, gain_second, shift_second = (
-        lax.all_gather(inner_weight, "fsdp", axis=0, tiled=True),
-        lax.all_gather(inner_bias, "fsdp", axis=0, tiled=True),
-        lax.all_gather(outer_weight, "fsdp", axis=0, tiled=True),
-        lax.all_gather(outer_bias, "fsdp", axis=0, tiled=True),
-        lax.all_gather(second_gain, "fsdp", axis=0, tiled=True),
-        lax.all_gather(second_shift, "fsdp", axis=0, tiled=True),
-    )
     inner_pre = forward_rows(first_low, inner_all) + inner_offset.astype(jnp.float32)
     active_low = exact_gelu(inner_pre).astype(jnp.bfloat16)
     second_sum = first_out + forward_rows(active_low, outer_all) + outer_offset.astype(jnp.float32)
@@ -260,98 +757,50 @@
         + backward_rows(value_img_grad, value_back)
     )
     grad_regions = region_input.reshape(image_count, region_slots, width_model)
-    (
-        query_weight_part,
-        key_weight_part,
-        value_weight_part,
-        out_weight_part,
-        query_bias_part,
-        value_bias_part,
-        out_bias_part,
-        first_gain_part,
-        first_shift_part,
-        inner_weight_part,
-        inner_bias_part,
-        outer_weight_part,
-        outer_bias_part,
-        second_gain_part,
-        second_shift_part,
-    ) = (
-        lax.psum_scatter(query_weight_grad, "fsdp", scatter_dimension=0, tiled=True),
-        lax.psum_scatter(key_weight_grad, "fsdp", scatter_dimension=0, tiled=True),
-        lax.psum_scatter(value_weight_grad, "fsdp", scatter_dimension=0, tiled=True),
-        lax.psum_scatter(out_weight_grad, "fsdp", scatter_dimension=0, tiled=True),
-        lax.psum_scatter(query_bias_grad, "fsdp", scatter_dimension=0, tiled=True),
-        lax.psum_scatter(value_bias_grad, "fsdp", scatter_dimension=0, tiled=True),
-        lax.psum_scatter(out_bias_grad, "fsdp", scatter_dimension=0, tiled=True),
-        lax.psum_scatter(first_gain_grad, "fsdp", scatter_dimension=0, tiled=True),
-        lax.psum_scatter(first_shift_grad, "fsdp", scatter_dimension=0, tiled=True),
-        lax.psum_scatter(inner_weight_grad, "fsdp", scatter_dimension=0, tiled=True),
-        lax.psum_scatter(inner_bias_grad, "fsdp", scatter_dimension=0, tiled=True),
-        lax.psum_scatter(outer_weight_grad, "fsdp", scatter_dimension=0, tiled=True),
-        lax.psum_scatter(outer_bias_grad, "fsdp", scatter_dimension=0, tiled=True),
-        lax.psum_scatter(second_gain_grad, "fsdp", scatter_dimension=0, tiled=True),
-        lax.psum_scatter(second_shift_grad, "fsdp", scatter_dimension=0, tiled=True),
-    )
-    (
-        query_weight_total,
-        key_weight_total,
-        value_weight_total,
-        out_weight_total,
-        query_bias_total,
-        value_bias_total,
-        out_bias_total,
-        first_gain_total,
-        first_shift_total,
-        inner_weight_total,
-        inner_bias_total,
-        outer_weight_total,
-        outer_bias_total,
-        second_gain_total,
-        second_shift_total,
-    ) = (
-        lax.psum(query_weight_part.astype(jnp.bfloat16), "rep").astype(jnp.float32),
-        lax.psum(key_weight_part.astype(jnp.bfloat16), "rep").astype(jnp.float32),
-        lax.psum(value_weight_part.astype(jnp.bfloat16), "rep").astype(jnp.float32),
-        lax.psum(out_weight_part.astype(jnp.bfloat16), "rep").astype(jnp.float32),
-        lax.psum(query_bias_part.astype(jnp.bfloat16), "rep").astype(jnp.float32),
-        lax.psum(value_bias_part.astype(jnp.bfloat16), "rep").astype(jnp.float32),
-        lax.psum(out_bias_part.astype(jnp.bfloat16), "rep").astype(jnp.float32),
-        lax.psum(first_gain_part.astype(jnp.bfloat16), "rep").astype(jnp.float32),
-        lax.psum(first_shift_part.astype(jnp.bfloat16), "rep").astype(jnp.float32),
-        lax.psum(inner_weight_part.astype(jnp.bfloat16), "rep").astype(jnp.float32),
-        lax.psum(inner_bias_part.astype(jnp.bfloat16), "rep").astype(jnp.float32),
-        lax.psum(outer_weight_part.astype(jnp.bfloat16), "rep").astype(jnp.float32),
-        lax.psum(outer_bias_part.astype(jnp.bfloat16), "rep").astype(jnp.float32),
-        lax.psum(second_gain_part.astype(jnp.bfloat16), "rep").astype(jnp.float32),
-        lax.psum(second_shift_part.astype(jnp.bfloat16), "rep").astype(jnp.float32),
-    )
+    matrix_totals, vector_totals = reduce_weights(
+        (
+            query_weight_grad,
+            key_weight_grad,
+            value_weight_grad,
+            out_weight_grad,
+            inner_weight_grad,
+            outer_weight_grad,
+        ),
+        (
+            query_bias_grad,
+            value_bias_grad,
+            out_bias_grad,
+            first_gain_grad,
+            first_shift_grad,
+            inner_bias_grad,
+            outer_bias_grad,
+            second_gain_grad,
+            second_shift_grad,
+        ),
+        use_kernels,
+    )
+    query_total, key_total, value_total, out_total, inner_total, outer_total = matrix_totals
     return (
         out_caption,
         out_region,
         grad_captions,
         grad_regions,
-        query_weight_total,
-        key_weight_total,
-        value_weight_total,
-        out_weight_total,
-        query_bias_total,
-        value_bias_total,
-        out_bias_total,
-        first_gain_total,
-        first_shift_total,
-        inner_weight_total,
-        inner_bias_total,
-        outer_weight_total,
-        outer_bias_total,
-        second_gain_total,
-        second_shift_total,
+        query_total,
+        key_total,
+        value_total,
+        out_total,
+        *vector_totals[:5],
+        inner_total,
+        vector_totals[5],
+        outer_total,
+        *vector_totals[6:],
     )
 
 
 def solution(mesh):
+    use_kernels = mesh.shape["fsdp"] == OWNERS
     return jax.shard_map(
-        on_device,
+        functools.partial(on_device, use_kernels),
         mesh=mesh,
         in_specs=(
             P(("fsdp", "rep"), None, None),

time: 1540 us -> 826 us (0.54)
  waiting for transfers between devices: 671 us -> 0 us
  Pallas kernels: 0 us -> 190 us
  blocking collectives: 157 us -> 0 us
  local copies, waits for them, and re-layouts: 164 us -> 127 us
  between operations: 17.9 us -> 1.6 us
    reduce_scatter x3 -> x0, waiting for transfers between devices: 349 us -> none  [the longest x1 175 us: on_device(): lax.psum_scatter(outer_weight_grad, 'fsdp', scatter_dimension=0, tiled=True)]
    unnamed x16 -> x0, waiting for transfers between devices: 249 us -> none
    pallas_call x0 -> x2, Pallas kernels: none -> 190 us  [the longest x1 113 us: reduce_all(): pl.pallas_call(functools.partial(reduce_kernel, splits, aligns, owners),...]
    unnamed x2 -> x0, blocking collectives: 155 us -> none
    all_gather x6 -> x0, waiting for transfers between devices: 73.1 us -> none  [the longest x1 51.3 us: on_device(): lax.all_gather(query_weight, 'fsdp', axis=0, tiled=True)]
    unnamed x149 -> x102, local copies, waits for them, and re-layouts: 60.3 us -> 28.6 us
    convert_element_type x24 -> x0, other arithmetic: 19.8 us -> none  [the longest x1 1.81 us: on_device(): lax.psum(inner_weight_part.astype(jnp.bfloat16), 'rep').astype(jnp.float32)]
    concatenate x6, local copies, waits for them, and re-layouts: 36.6 us -> 17.1 us  [sequence_rows(): joined = jnp.concatenate([caption_block, image_block], axis=1)]
  transfers between devices with their start and end apart: 13 -> 0, of which waited for: 7 -> 0; matrix products, arithmetic and copies ran while one was open for 36% -> 0% of each run, Pallas kernels for 0% -> 0%
where the time goes in v1:
time: 826 us; the launch traced here: 817 us
  matrix products  408 us (49%)
  Pallas kernels  190 us (23%)
  local copies, waits for them, and re-layouts  127 us (15%)
  other arithmetic  91.2 us (11%)
    dot_general x9, matrix products, forward_rows(): return jnp.dot(row_block, weight, preferred_element_type=jnp.float32)  132 us
    pallas_call x1, Pallas kernels, reduce_all(): pl.pallas_call(functools.partial(reduce_kernel, splits, aligns, owners),...  113 us
    dot_general x9, matrix products, backward_rows(): lax.dot_general(gradient, weight, (((1,), (1,)), ((), ())), preferred_ele...  91.4 us
    pallas_call x1, Pallas kernels, gather_all(): pl.pallas_call(functools.partial(gather_kernel, splits, aligns), out_shap...  76.2 us
    dot_general x9, matrix products, weight_grad(): lax.dot_general(row_block, gradient, (((0,), (0,)), ((), ())), preferred_...  59.1 us
    unnamed x102, local copies, waits for them, and re-layouts  28.6 us
    convert_element_type x1, other arithmetic, on_device(): score_grad = (probs_again * (probs_grad - row_inner)).astype(jnp.bfloat16)  27.5 us
    dot_general x1, matrix products, on_device(): jnp.einsum('sqhe,skhe->shqk', context_grad, values_seq, preferred_element...  25.3 us

profile of v1, /device:TPU:0, one launch (start us, length us, event | category | flops | bytes accessed | tf_op | source)
XLA Modules:
  0.0 816.7 jit_solution(2492212841286604413)
XLA Ops:
  15.7 76.2 %gather_rows.1 = (bf16[768,3072]{1,0:T(8,128)(2,1)}, bf16[768,3072]{1,0:T(8,128)(2,1)}, bf16[3072,768]{1,0:T(8,128)(2,1)}, f32[256,128]{1,0:T(8,128)}) custom-call(bf16[48,3072]{1,0:T(8,128)(2,1)} %pad_maximum_fusion.16.refs_0_, bf16[48,3072]{1,0:T(8,128)(2,1)} %refs_1_.1, bf16[192,768]{1,0:T(8,128)(2,1)} %refs_2_.1, f32[16,128]{1,0:T(8,128)} %bitcast.235), custom_call_target="tpu_custom_call" | custom-call | tf_op jit(solution)/shard_map/gather_rows/pallas_call | solution.py:247
  151.1 15.9 %fusion.6 = (f32[10,12,256]{2,1,0:T(8,128)S(1)}, f32[10,12,256,256]{2,3,1,0:T(8,128)}) fusion(pred[10,256]{1,0:T(8,128)(4,1)S(1)} %get-tuple-element.82, bf16[10,128,12,64]{1,3,2,0:T(8,128)(2,1)} %bitcast.215, bf16[10,128,12,64]{1,3,2,0:T(8,128)(2,1)} %copy.123, bf16[10,128,12,64]{1,3,2,0:T(8,128)(2,1)} %bitcast.210, bf16[10,128,12,64]{1,3,2,0:T(8,128)(2,1)} %copy.120), kind=kOutput, calls=%fused_computation.23 | convolution fusion | flops 1045923840 | bytes 39447040 | tf_op jit(solution)/shard_map/sqhe,skhe->shqk/dot_general | solution.py:649
  166.9 15.4 %exponential_reduce_fusion = f32[10,12,256]{2,1,0:T(8,128)S(1)} fusion(f32[10,12,256,256]{2,3,1,0:T(8,128)} %get-tuple-element.84, f32[10,12,256]{2,1,0:T(8,128)S(1)} %get-tuple-element.83, pred[10,256]{1,0:T(8,128)(4,1)S(1)} %get-tuple-element.82), kind=kLoop, calls=%fused_computation.20 | loop fusion | flops 31426560 | bytes 31705600 | tf_op jit(solution)/shard_map/reduce_sum | solution.py:656
  182.5 15.9 %convert_bitcast_fusion = bf16[10,256,12,64]{1,3,2,0:T(8,128)(2,1)} fusion(bf16[10,128,12,64]{1,3,2,0:T(8,128)(2,1)} %bitcast.212, bf16[10,128,12,64]{1,3,2,0:T(8,128)(2,1)S(1)} %copy-done.10, f32[10,12,256,256]{2,3,1,0:T(8,128)} %get-tuple-element.84, f32[10,12,256]{2,1,0:T(8,128)S(1)} %log_add_fusion, pred[10,256]{1,0:T(8,128)(4,1)S(1)} %get-tuple-element.82), kind=kOutput, calls=%fused_computation.69 | convolution fusion | flops 1047920640 | bytes 39447040 | tf_op jit(solution)/shard_map/shqk,skhe->sqhe/dot_general | solution.py:658
  198.4 5.2 copy.125
  206.4 6.3 fusion.97
  215.9 84.6 %multiply_convert_fusion.1 = (bf16[2560,3072]{1,0:T(8,128)(2,1)}, f32[2560,3072]{1,0:T(8,128)}, f32[2560,3072]{1,0:T(8,128)}) fusion(f32[3072]{0:T(1024)S(1)} %copy-done.41, bf16[768,3072]{1,0:T(8,128)(2,1)S(1)} %bitcast.246, f32[2560,768]{1,0:T(8,128)S(1)} %get-tuple-element.86, f32[768]{0:T(1024)S(1)} %add.191, f32[768]{0:T(1024)S(1)} %mul.187, ...), kind=kOutput, calls=%fused_computation.6 | convolution fusion | flops 12608471040 | bytes 91265024 | tf_op jit(solution)/shard_map/dot_general | solution.py:30
  300.5 19.6 %fusion.98 = (f32[2560]{0:T(1024)S(1)}, f32[2560,768]{1,0:T(8,128)S(1)}) fusion(f32[768]{0:T(1024)S(1)} %copy-done.42, bf16[2560,3072]{1,0:T(8,128)(2,1)} %get-tuple-element.52, bf16[3072,768]{1,0:T(8,128)(2,1)} %get-tuple-element.30, f32[768]{0:T(1024)S(1)} %add.191, f32[768]{0:T(1024)S(1)} %mul.187, f32[2560]{0:T(1024)S(1)} %fusion.54, ...), kind=kOutput, calls=%fused_computation.193 | convolution fusion | flops 12093356032 | bytes 36215808 | tf_op jit(solution)/shard_map/dot_general | solution.py:30
  330.0 7.4 fusion.91
  343.0 37.2 %convert_reduce_fusion = (f32[3072]{0:T(1024)S(1)}, bf16[2560,3072]{1,0:T(8,128)(2,1)}) fusion(f32[2560,3072]{1,0:T(8,128)} %get-tuple-element.53, bf16[2560,768]{1,0:T(8,128)(2,1)} %get-tuple-element.41, bf16[3072,768]{1,0:T(8,128)(2,1)} %get-tuple-element.30, f32[2560,3072]{1,0:T(8,128)} %get-tuple-element.87, f32[3072]{0:T(1024)S(1)} %copy-done.41), kind=kOutput, calls=%fused_computation.2 | convolution fusion | flops 12213285888 | bytes 87318528 | tf_op jit(solution)/shard_map/dot_general | solution.py:34
  380.2 18.7 %convolution_convert_fusion.refs_2_ = bf16[3072,768]{1,0:T(8,128)(2,1)} fusion(bf16[2560,3072]{1,0:T(8,128)(2,1)} %get-tuple-element.52, bf16[2560,768]{1,0:T(8,128)(2,1)} %get-tuple-element.41), kind=kOutput, calls=%fused_computation.48 | convolution fusion | flops 12081954816 | bytes 24379392 | tf_op jit(solution)/shard_map/dot_general | solution.py:40
  398.9 25.1 %multiply_reduce_fusion.3 = (f32[768]{0:T(1024)S(1)}, f32[2560]{0:T(1024)S(1)}, f32[768]{0:T(1024)S(1)}, f32[2560,768]{1,0:T(8,128)}) fusion(f32[2560,768]{1,0:T(8,128)} %copy-done.4, f32[2560]{0:T(1024)S(1)} %fusion.54, f32[2560]{0:T(1024)S(1)} %broadcast_multiply_fusion.3, f32[768]{0:T(1024)S(1)} %mul.187, bf16[2560,3072]{1,0:T(8,128)(2,1)} %get-tuple-element.98, ...), kind=kOutput, calls=%fused_computation.33 | convolution fusion | flops 12099251200 | bytes 44090368 | tf_op jit(solution)/shard_map/dot_general | solution.py:34
  424.0 7.2 fusion.90
  431.2 21.7 %convolution_convert_fusion.1.refs_1_ = bf16[768,3072]{1,0:T(8,128)(2,1)} fusion(bf16[2560,3072]{1,0:T(8,128)(2,1)} %get-tuple-element.98, f32[2560,768]{1,0:T(8,128)} %copy-done.4, f32[768]{0:T(1024)S(1)} %add.191, f32[768]{0:T(1024)S(1)} %mul.187, f32[2560]{0:T(1024)S(1)} %fusion.54, f32[2560]{0:T(1024)S(1)} %broadcast_multiply_fusion.3), kind=kOutput, calls=%fused_computation.49 | convolution fusion | flops 12091785216 | bytes 28338176 | tf_op jit(solution)/shard_map/dot_general | solution.py:40
  462.7 8.7 %convolution_convert_fusion.2 = bf16[2560,768]{1,0:T(8,128)(2,1)} fusion(bf16[768,3072]{1,0:T(8,128)(2,1)} %get-tuple-element.27, f32[2560,768]{1,0:T(8,128)} %copy-done.2), kind=kOutput, calls=%fused_computation.50 | convolution fusion | flops 3023831040 | bytes 12976128 | tf_op jit(solution)/shard_map/dot_general | solution.py:34
  471.4 12.7 %reshape.393 = bf16[10,256,12,64]{3,2,1,0:T(8,128)(2,1)} reshape(bf16[2560,768]{1,0:T(8,128)(2,1)} %convolution_convert_fusion.2) | data formatting | bytes 7864320 | tf_op jit(solution)/shard_map/reshape | solution.py:701
  484.1 11.5 %copy.127 = bf16[10,256,12,64]{1,3,2,0:T(8,128)(2,1)} copy(bf16[10,256,12,64]{3,2,1,0:T(8,128)(2,1)} %reshape.393) | data formatting | bytes 7864320 | tf_op jit(solution)/shard_map/reshape | solution.py:701
  495.6 17.7 %fusion.51 = f32[10,12,64,256]{3,2,1,0:T(8,128)} fusion(bf16[10,256,12,64]{1,3,2,0:T(8,128)(2,1)} %copy.127, f32[10,12,256,256]{2,3,1,0:T(8,128)} %get-tuple-element.84, f32[10,12,256]{2,1,0:T(8,128)S(1)} %copy-done.27, pred[10,256]{1,0:T(8,128)(4,1)S(1)} %copy-done.34), kind=kOutput, calls=%fused_computation.127 | convolution fusion | flops 1038090240 | bytes 43379200 | tf_op jit(solution)/shard_map/shqk,sqhe->skhe/dot_general | solution.py:707
  513.3 6.0 convert_reduce_fusion.3
  526.6 5.8 copy.175
  532.4 5.6 convert_reduce_fusion.5
  540.1 6.0 fusion.93
  551.4 25.3 %multiply_reduce_fusion = (f32[10,12,256]{2,1,0:T(8,128)}, f32[10,12,256,256]{2,3,1,0:T(8,128)}) fusion(f32[10,12,256,256]{2,3,1,0:T(8,128)} %get-tuple-element.84, f32[10,12,256]{2,1,0:T(8,128)S(1)} %copy-done.28, pred[10,256]{1,0:T(8,128)(4,1)S(1)} %copy-done.34, bf16[10,256,12,64]{1,3,2,0:T(8,128)(2,1)S(1)} %copy-done.8, ...), kind=kOutput, calls=%fused_computation.4 | convolution fusion | flops 1053788160 | bytes 71027200 | tf_op jit(solution)/shard_map/sqhe,skhe->shqk/dot_general | solution.py:704
  576.7 27.5 %multiply_convert_fusion = bf16[10,12,256,256]{2,3,1,0:T(8,128)(2,1)} fusion(f32[10,12,256,256]{2,3,1,0:T(8,128)} %get-tuple-element.92, f32[10,12,256,256]{2,3,1,0:T(8,128)} %get-tuple-element.84, f32[10,12,256]{2,1,0:T(8,128)} %get-tuple-element.91, f32[10,12,256]{2,1,0:T(8,128)} %copy-done.26, pred[10,256]{1,0:T(8,128)(4,1)S(1)} %copy-done.34), kind=kLoop, calls=%fused_computation.3 | loop fusion | flops 47185920 | bytes 78891520 | tf_op jit(solution)/shard_map/convert_element_type | solution.py:714
  604.2 11.5 %broadcast_multiply_fusion = f32[10,12,64,256]{3,2,1,0:T(8,128)} fusion(bf16[10,12,256,256]{2,3,1,0:T(8,128)(2,1)} %multiply_convert_fusion, bf16[10,128,12,64]{1,3,2,0:T(8,128)(2,1)} %bitcast.211, bf16[10,128,12,64]{1,3,2,0:T(8,128)(2,1)S(1)} %copy-done.9), kind=kOutput, calls=%fused_computation.66 | convolution fusion | flops 1016463360 | bytes 27525120 | tf_op jit(solution)/shard_map/shqk,sqhe->skhe/dot_general | solution.py:720
  615.7 9.5 %broadcast_multiply_fusion.1 = f32[10,12,64,256]{3,2,1,0:T(8,128)S(1)} fusion(bf16[10,12,256,256]{2,3,1,0:T(8,128)(2,1)} %multiply_convert_fusion, bf16[10,128,12,64]{1,3,2,0:T(8,128)(2,1)} %bitcast.216, bf16[10,128,12,64]{1,3,2,0:T(8,128)(2,1)} %copy.123), kind=kOutput, calls=%fused_computation.67 | convolution fusion | flops 1016463360 | bytes 27525120 | tf_op jit(solution)/shard_map/shqk,skhe->sqhe/dot_general | solution.py:716
  653.2 5.5 fusion.14
  664.1 6.0 copy.174
  670.2 5.4 convolution_convert_fusion.10
  676.2 5.9 copy.173
  682.1 5.6 convert_reduce_fusion.6
  693.1 113.4 %reduce_rows.1 = (f32[48,3072]{1,0:T(8,128)S(1)}, f32[48,3072]{1,0:T(8,128)S(1)}, f32[192,768]{1,0:T(8,128)S(1)}, f32[16,128]{1,0:T(8,128)S(1)}) custom-call(bf16[768,3072]{1,0:T(8,128)(2,1)} %pad_maximum_fusion.refs_0_, bf16[768,3072]{1,0:T(8,128)(2,1)} %convolution_convert_fusion.1.refs_1_, bf16[3072,768]{1,0:T(8,128)(2,1)} %convolution_convert_fusion.refs_2_, ...), custom_call_target="tpu_custom_call" | custom-call | tf_op jit(solution)/shard_map/reduce_rows/pallas_call | solution.py:461
  (199 shorter events, 169.0 us)
Async XLA Ops:
  0.7 12.8 %copy-start.23 = (bf16[10,128,768]{2,1,0:T(8,128)(2,1)S(1)}, bf16[10,128,768]{2,1,0:T(8,128)(2,1)}, u32[]{:S(2)}) copy-start(bf16[10,128,768]{2,1,0:T(8,128)(2,1)} %param.22) | copy-start | bytes 5898244
  5.3 177.2 %copy-start.33 = (pred[10,256]{1,0:T(8,128)(4,1)}, pred[10,256]{1,0:T(8,128)(4,1)S(1)}, u32[]{:S(2)}) copy-start(pred[10,256]{1,0:T(8,128)(4,1)S(1)} %get-tuple-element.82) | copy-start | bytes 7684
  130.0 5.6 copy-start.37
  166.9 15.5 %copy-start.10 = (bf16[10,128,12,64]{1,3,2,0:T(8,128)(2,1)S(1)}, bf16[10,128,12,64]{1,3,2,0:T(8,128)(2,1)}, u32[]{:S(2)}) copy-start(bf16[10,128,12,64]{1,3,2,0:T(8,128)(2,1)} %copy.117) | copy-start | bytes 5898244
  182.5 16.0 %copy-start.26 = (f32[10,12,256]{2,1,0:T(8,128)}, f32[10,12,256]{2,1,0:T(8,128)S(1)}, u32[]{:S(2)}) copy-start(f32[10,12,256]{2,1,0:T(8,128)S(1)} %log_add_fusion) | copy-start | bytes 368644
  198.4 8.0 copy-start.16
  198.4 8.0 copy-start.43
  206.4 6.3 copy-start.14
  206.4 9.5 %slice-start.2 = ((s8[4718592]{0:T(1024)(128)(4,1)}), s8[4194304]{0:T(1024)(128)(4,1)S(1)}, s32[]{:S(2)}) async-start(s8[4718592]{0:T(1024)(128)(4,1)} %bitcast.245), calls=%async_computation.2 | async-start | bytes 8388608
  206.4 9.5 %slice-start.3 = ((s8[4718592]{0:T(1024)(128)(4,1)}), s8[524288]{0:T(1024)(128)(4,1)S(1)}, s32[]{:S(2)}) async-start(s8[4718592]{0:T(1024)(128)(4,1)} %bitcast.245), calls=%async_computation.3 | async-start | bytes 1048576
  212.7 87.8 %copy-start.4 = (f32[2560,768]{1,0:T(8,128)}, f32[2560,768]{1,0:T(8,128)S(1)}, u32[]{:S(2)}) copy-start(f32[2560,768]{1,0:T(8,128)S(1)} %get-tuple-element.86) | copy-start | bytes 23592964
  215.9 84.6 %copy-start.42 = (f32[768]{0:T(1024)S(1)}, f32[768]{0:T(1024)}, u32[]{:S(2)}) copy-start(f32[768]{0:T(1024)} %add.198) | copy-start | bytes 9220
  320.1 9.1 %copy-start.1 = (f32[2560,768]{1,0:T(8,128)}, f32[2560,768]{1,0:T(8,128)S(1)}, u32[]{:S(2)}) copy-start(f32[2560,768]{1,0:T(8,128)S(1)} %get-tuple-element.89) | copy-start | bytes 23592964
  322.0 7.9 copy-start.39
  337.4 5.6 copy-start.3
  398.9 25.1 %copy-start.32 = (f32[2560]{0:T(1024)S(1)}, f32[2560]{0:T(1024)}, u32[]{:S(2)}) copy-start(f32[2560]{0:T(1024)} %copy-done.31) | copy-start | bytes 30724
  484.1 11.5 %copy-start.27 = (f32[10,12,256]{2,1,0:T(8,128)S(1)}, f32[10,12,256]{2,1,0:T(8,128)}, u32[]{:S(2)}) copy-start(f32[10,12,256]{2,1,0:T(8,128)} %copy-done.26) | copy-start | bytes 368644
  484.1 11.5 %copy-start.34 = (pred[10,256]{1,0:T(8,128)(4,1)S(1)}, pred[10,256]{1,0:T(8,128)(4,1)}, u32[]{:S(2)}) copy-start(pred[10,256]{1,0:T(8,128)(4,1)} %copy-done.33) | copy-start | bytes 7684
  526.6 5.8 copy-start.38
  532.4 5.6 copy-start.20
  546.1 5.3 copy-start.28
  576.7 27.5 %copy-start.9 = (bf16[10,128,12,64]{1,3,2,0:T(8,128)(2,1)S(1)}, bf16[10,128,12,64]{1,3,2,0:T(8,128)(2,1)}, u32[]{:S(2)}) copy-start(bf16[10,128,12,64]{1,3,2,0:T(8,128)(2,1)} %copy.120) | copy-start | bytes 5898244
  644.7 8.0 copy-start.13
  648.9 9.8 %slice-start = ((s8[7864320]{0:T(1024)(128)(4,1)}), s8[4194304]{0:T(1024)(128)(4,1)S(1)}, s32[]{:S(2)}) async-start(s8[7864320]{0:T(1024)(128)(4,1)} %bitcast.202), calls=%async_computation | async-start | bytes 8388608
  653.1 5.5 slice-start.1
  653.2 5.5 copy-start.24
  670.2 5.4 copy-start.21
  682.1 5.7 copy-start.19
  682.1 6.2 copy-start.40
  682.1 6.8 copy-start.29
  693.1 115.5 %copy-start.18 = (f32[2,128,768]{2,1,0:T(8,128)S(1)}, f32[2,128,768]{2,1,0:T(8,128)}, u32[]{:S(2)}) copy-start(f32[2,128,768]{2,1,0:T(8,128)} %copy.136) | copy-start | bytes 2359300
  693.1 119.1 %copy-start.25 = (bf16[2,128,768]{2,1,0:T(8,128)(2,1)S(1)}, bf16[2,128,768]{2,1,0:T(8,128)(2,1)}, u32[]{:S(2)}) copy-start(bf16[2,128,768]{2,1,0:T(8,128)(2,1)} %copy.142) | copy-start | bytes 1179652
  (16 other events, 63.4 us)

commit v2 on v1

--- a/solution.py
+++ b/solution.py
@@ -7,44 +7,8 @@
 from jax.experimental.pallas import tpu as pltpu
 from jax.sharding import PartitionSpec as P
 
-HEADS = 12
-
-
 EPSILON = 1e-12
 MASKED_SCORE = -1e30
-HIGHEST_PRECISION = lax.Precision.HIGHEST
-
-
-def normalize(values, norm_gain, norm_shift):
-    average = jnp.mean(values, axis=-1, keepdims=True)
-    centred = values - average
-    spread = jnp.mean(centred * centred, axis=-1, keepdims=True)
-    return centred * lax.rsqrt(spread + EPSILON) * norm_gain + norm_shift
-
-
-def exact_gelu(values):
-    return jax.nn.gelu(values, approximate=False)
-
-
-def forward_rows(row_block, weight):
-    return jnp.dot(row_block, weight, preferred_element_type=jnp.float32)
-
-
-def backward_rows(gradient, weight):
-    return lax.dot_general(
-        gradient, weight, (((1,), (1,)), ((), ())), preferred_element_type=jnp.float32
-    )
-
-
-def weight_grad(row_block, gradient):
-    return lax.dot_general(
-        row_block, gradient, (((0,), (0,)), ((), ())), preferred_element_type=jnp.float32
-    )
-
-
-def column_sum(gradient):
-    return jnp.sum(gradient.astype(jnp.float32), axis=0)
-
 
 MESH = pl.DeviceIdType.MESH
 PLANES = 4
@@ -511,34 +475,486 @@
     return vectors
 
 
-def gather_weights(matrices, vectors, use_kernels):
+def gather_weights(squares, inner, outer, vectors, use_kernels):
+    square = jnp.concatenate(squares, axis=1)
     if not use_kernels:
-        whole = [lax.all_gather(m, "fsdp", axis=0, tiled=True) for m in (*matrices, *vectors)]
-        return whole[: len(matrices)], whole[len(matrices) :]
-    square = jnp.concatenate(matrices[:4], axis=1)
+        whole = [lax.all_gather(m, "fsdp", axis=0, tiled=True) for m in (square, inner, outer)]
+        return *whole, [lax.all_gather(v, "fsdp", axis=0, tiled=True) for v in vectors]
     packed = pack_vectors(vectors, 1)
     square, inner, outer, packed = gather_all(
-        (square, matrices[4], matrices[5], packed), WEIGHT_SPLITS, OWNERS, 1
-    )
-    whole_vectors = unpack_vectors(packed, OWNERS, [v.shape[0] for v in vectors])
-    return [*jnp.split(square, 4, axis=1), inner, outer], whole_vectors
-
-
-def reduce_weights(matrices, vectors, use_kernels):
+        (square, inner, outer, packed), WEIGHT_SPLITS, OWNERS, 1
+    )
+    return square, inner, outer, unpack_vectors(packed, OWNERS, [v.shape[0] for v in vectors])
+
+
+def reduce_weights(square, inner, outer, vectors, use_kernels):
     if not use_kernels:
         totals = []
-        for part in (*matrices, *vectors):
-            share = lax.psum_scatter(part, "fsdp", scatter_dimension=0, tiled=True)
+        for part in (square, inner, outer, *vectors):
+            wide = part.astype(jnp.float32)
+            share = lax.psum_scatter(wide, "fsdp", scatter_dimension=0, tiled=True)
             totals.append(lax.psum(share.astype(jnp.bfloat16), "rep").astype(jnp.float32))
-        return totals[: len(matrices)], totals[len(matrices) :]
-    low = [m.astype(jnp.bfloat16) for m in matrices]
-    square = jnp.concatenate(low[:4], axis=1)
+        return *totals[:3], totals[3:]
     packed = pack_vectors(vectors, OWNERS)
     square, inner, outer, packed = reduce_all(
-        (square, low[4], low[5], packed), WEIGHT_SPLITS, OWNERS, 2
+        (square, inner, outer, packed), WEIGHT_SPLITS, OWNERS, 2
     )
     sizes = [v.shape[0] // OWNERS for v in vectors]
-    return [*jnp.split(square, 4, axis=1), inner, outer], unpack_vectors(packed, 1, sizes)
+    return square, inner, outer, unpack_vectors(packed, 1, sizes)
+
+
+def dot_nn(left, right):
+    return lax.dot_general(
+        left, right, (((1,), (0,)), ((), ())), preferred_element_type=jnp.float32
+    )
+
+
+def dot_nt(left, right):
+    return lax.dot_general(
+        left, right, (((1,), (1,)), ((), ())), preferred_element_type=jnp.float32
+    )
+
+
+def dot_tn(left, right):
+    return lax.dot_general(
+        left, right, (((0,), (0,)), ((), ())), preferred_element_type=jnp.float32
+    )
+
+
+HEAD = 64
+EXTRA_ROWS = 16
+HEADS_AT_ONCE = 2
+
+
+def key_mask_rows(length, count, slots):
+    slot = lax.broadcasted_iota(jnp.int32, (EXTRA_ROWS, 2 * slots), 1)
+    row = lax.broadcasted_iota(jnp.int32, (EXTRA_ROWS, 2 * slots), 0)
+    live = (slot < length) | ((slot >= slots) & (slot < slots + count))
+    return jnp.where((row > 0) | live, 0.0, MASKED_SCORE).astype(jnp.bfloat16)
+
+
+def query_mask_rows(slots):
+    row = lax.broadcasted_iota(jnp.int32, (EXTRA_ROWS, 2 * slots), 0)
+    return jnp.where(row == 0, 1.0, 0.0).astype(jnp.bfloat16)
+
+
+def live_rows_column(length, count, slots):
+    row = lax.broadcasted_iota(jnp.int32, (2 * slots, 1), 0)
+    live = (row < length) | ((row >= slots) & (row < slots + count))
+    return jnp.where(live, 1.0, 0.0)
+
+
+def head_rows(cap_part, image_part, base):
+    rows = pl.ds(pl.multiple_of(base, HEAD), HEAD)
+    return jnp.concatenate([cap_part[rows, :], image_part[rows, :]], axis=1)
+
+
+def project_kernel(length_ref, count_ref, group_ref, cap_ref, image_ref, weight_ref, bias_ref,
+                   cap_out, image_out, context_out, lse_out, weight_turned, bias_wide):
+    step = pl.program_id(0)
+    width = cap_ref.shape[2]
+    slots = cap_ref.shape[1]
+    scaling = HEAD ** (-0.5)
+
+    @pl.when(step == 0)
+    def _():
+        weight_turned[...] = weight_ref[:, : 3 * width].T
+        bias_wide[...] = jnp.broadcast_to(bias_ref[...], (128, 3 * width)).T
+
+    def project(rows):
+        parts = []
+        for part in range(3):
+            turned = dot_nt(weight_turned[part * width : (part + 1) * width, :], rows)
+            bias = bias_wide[part * width : (part + 1) * width, :]
+            turned = turned + jnp.concatenate([bias, bias], axis=1)
+            turned = turned.astype(jnp.bfloat16)
+            parts.append(turned * scaling if part == 0 else turned)
+        return parts
+
+    @pl.when(step == 0)
+    def _():
+        parts = project(image_ref[...].reshape(2 * slots, width))
+        for part in range(3):
+            rows = slice(part * width, (part + 1) * width)
+            image_out[0, rows, :] = parts[part][:, :slots]
+            image_out[1, rows, :] = parts[part][:, slots:]
+
+    @pl.when(lax.rem(step, 2) == 0)
+    def _():
+        parts = project(cap_ref[...].reshape(2 * slots, width))
+        for part in range(3):
+            rows = slice(part * width, (part + 1) * width)
+            cap_out[0, rows, :] = parts[part][:, :slots]
+            cap_out[1, rows, :] = parts[part][:, slots:]
+
+    cap_part = cap_out.at[lax.rem(step, 2)]
+    image_part = image_out.at[group_ref[step]]
+    key_extra = key_mask_rows(length_ref[step], count_ref[step], slots)
+    query_extra = query_mask_rows(slots)
+
+    def heads(turn, carry):
+        for inner in range(HEADS_AT_ONCE):
+            head = turn * HEADS_AT_ONCE + inner
+            query = head_rows(cap_part, image_part, head * HEAD)
+            key = head_rows(cap_part, image_part, width + head * HEAD)
+            value = head_rows(cap_part, image_part, 2 * width + head * HEAD)
+            scores = dot_tn(
+                jnp.concatenate([key, key_extra], axis=0),
+                jnp.concatenate([query, query_extra], axis=0),
+            )
+            largest = jnp.max(scores, axis=0, keepdims=True)
+            powers = jnp.exp(scores - largest)
+            total = jnp.sum(powers, axis=0, keepdims=True)
+            probs = (powers * (1.0 / total)).astype(jnp.bfloat16)
+            context = dot_nn(value, probs)
+            context_out[0, pl.ds(pl.multiple_of(head * HEAD, HEAD), HEAD), :] = context.astype(
+                jnp.bfloat16
+            )
+            lse_out[0, pl.ds(head, 1), :] = largest + jnp.log(total)
+        return carry
+
+    lax.fori_loop(0, width // HEAD // HEADS_AT_ONCE, heads, 0)
+
+
+def attend_forward(lengths, counts, groups, captions, regions, square, bias_row):
+    seqs, slots, width = captions.shape
+    images = regions.shape[0]
+    heads = width // HEAD
+    grid_spec = pltpu.PrefetchScalarGridSpec(
+        num_scalar_prefetch=3,
+        grid=(seqs,),
+        in_specs=[
+            pl.BlockSpec((2, slots, width), lambda s, *_: (s // 2, 0, 0)),
+            pl.BlockSpec((images, slots, width), lambda s, *_: (0, 0, 0)),
+            pl.BlockSpec(square.shape, lambda s, *_: (0, 0), pipeline_mode=pl.Buffered(1)),
+            pl.BlockSpec(bias_row.shape, lambda s, *_: (0, 0)),
+        ],
+        out_specs=[
+            pl.BlockSpec((2, 3 * width, slots), lambda s, *_: (s // 2, 0, 0)),
+            pl.BlockSpec((images, 3 * width, slots), lambda s, *_: (0, 0, 0)),
+            pl.BlockSpec((1, width, 2 * slots), lambda s, *_: (s, 0, 0)),
+            pl.BlockSpec((1, heads, 2 * slots), lambda s, *_: (s, 0, 0)),
+        ],
+        scratch_shapes=[
+            pltpu.VMEM((3 * width, width), jnp.bfloat16),
+            pltpu.VMEM((3 * width, 128), jnp.float32),
+        ],
+    )
+    return pl.pallas_call(
+        project_kernel,
+        grid_spec=grid_spec,
+        out_shape=[
+            jax.ShapeDtypeStruct((seqs, 3 * width, slots), jnp.bfloat16),
+            jax.ShapeDtypeStruct((images, 3 * width, slots), jnp.bfloat16),
+            jax.ShapeDtypeStruct((seqs, width, 2 * slots), jnp.bfloat16),
+            jax.ShapeDtypeStruct((seqs, heads, 2 * slots), jnp.float32),
+        ],
+        compiler_params=pltpu.CompilerParams(vmem_limit_bytes=48 * 1024 * 1024),
+        name="attend_forward",
+    )(lengths, counts, groups, captions, regions, square, bias_row)
+
+
+PHI_SLOPE = 0.2316419
+PHI_TERMS = (0.319381530, -0.356563782, 1.781477937, -1.821255978, 1.330274429)
+FF_CHUNK = 512
+
+
+def gelu_both(values):
+    density = 0.3989422804014327 * jnp.exp(-0.5 * values * values)
+    ratio = 1.0 / (1.0 + PHI_SLOPE * jnp.abs(values))
+    tail = PHI_TERMS[4]
+    for term in PHI_TERMS[3::-1]:
+        tail = tail * ratio + term
+    tail = tail * ratio * density
+    below = jnp.where(values >= 0.0, 1.0 - tail, tail)
+    return values * below, below + values * density
+
+
+def norm_parts(values):
+    average = jnp.mean(values, axis=-1, keepdims=True)
+    centred = values - average
+    spread = jnp.mean(centred * centred, axis=-1, keepdims=True)
+    inverse = lax.rsqrt(spread + EPSILON)
+    return centred * inverse, inverse
+
+
+def norm_back(gradient, gain, normal, inverse):
+    scaled = gradient * gain
+    first = jnp.mean(scaled, axis=-1, keepdims=True)
+    second = jnp.mean(scaled * normal, axis=-1, keepdims=True)
+    return (scaled - first - normal * second) * inverse
+
+
+def feed_kernel(length_ref, count_ref, group_ref, context_ref, cap_ref, image_ref, cap_cot_ref,
+                region_cot_ref, out_weight_ref, inner_ref, outer_ref, vector_ref, inner_bias_ref,
+                out_cap_ref, out_region_ref, cap_sum_ref, region_sum_ref, context_grad_ref,
+                out_grad_ref, inner_grad_ref, outer_grad_ref, vector_grad_ref, bias_grad_ref,
+                active_sc, slope_sc, inner_acc, outer_acc, out_acc):
+    step = pl.program_id(0)
+    slots = cap_ref.shape[1]
+    hidden = inner_ref.shape[1]
+    chunks = [slice(start, start + FF_CHUNK) for start in range(0, hidden, FF_CHUNK)]
+
+    @pl.when(step == 0)
+    def _():
+        inner_acc[...] = jnp.zeros_like(inner_acc)
+        outer_acc[...] = jnp.zeros_like(outer_acc)
+        out_acc[...] = jnp.zeros_like(out_acc)
+        vector_grad_ref[...] = jnp.zeros_like(vector_grad_ref)
+        bias_grad_ref[...] = jnp.zeros_like(bias_grad_ref)
+
+    def vector(row):
+        return vector_ref[row : row + 1, :]
+
+    def add_vector(row, values):
+        vector_grad_ref[row : row + 1, :] += jnp.sum(values, axis=0, keepdims=True)
+
+    live = live_rows_column(length_ref[step], count_ref[step], slots)
+    rows_in = jnp.concatenate([cap_ref[0], image_ref[0]], axis=0).astype(jnp.float32)
+    first_sum = rows_in + dot_tn(context_ref[0], out_weight_ref[...]) + vector(0)
+    first_normal, first_inverse = norm_parts(first_sum)
+    first_out = first_normal * vector(1) + vector(2)
+    first_low = first_out.astype(jnp.bfloat16)
+    second_sum = first_out + vector(3)
+    for chunk in chunks:
+        pre = dot_nn(first_low, inner_ref[:, chunk]) + inner_bias_ref[:, chunk]
+        active, slope = gelu_both(pre)
+        active = active.astype(jnp.bfloat16)
+        active_sc[:, chunk] = active
+        slope_sc[:, chunk] = slope
+        second_sum = second_sum + dot_nn(active, outer_ref[chunk, :])
+    second_normal, second_inverse = norm_parts(second_sum)
+    result = ((second_normal * vector(4) + vector(5)) * live).astype(jnp.bfloat16)
+    out_cap_ref[0] = result[:slots]
+    out_region_ref[0] = result[slots:]
+    cot = jnp.concatenate([cap_cot_ref[0], region_cot_ref[0]], axis=0).astype(jnp.float32) * live
+    add_vector(4, cot * second_normal)
+    add_vector(5, cot)
+    second_grad = norm_back(cot, vector(4), second_normal, second_inverse)
+    outer_grad = second_grad.astype(jnp.bfloat16)
+    add_vector(3, outer_grad.astype(jnp.float32))
+    first_grad = second_grad
+    first_turned = first_low.T
+    for chunk in chunks:
+        active_grad = dot_nt(outer_grad, outer_ref[chunk, :])
+        inner_grad = (active_grad * slope_sc[:, chunk]).astype(jnp.bfloat16)
+        bias_grad_ref[:, chunk] += jnp.sum(inner_grad.astype(jnp.float32), axis=0, keepdims=True)
+        inner_acc[:, chunk] += dot_nn(first_turned, inner_grad)
+        outer_acc[chunk, :] += dot_tn(active_sc[:, chunk], outer_grad)
+        first_grad = first_grad + dot_nt(inner_grad, inner_ref[:, chunk])
+    add_vector(1, first_grad * first_normal)
+    add_vector(2, first_grad)
+    sum_grad = norm_back(first_grad, vector(1), first_normal, first_inverse)
+    cap_sum_ref[0] = sum_grad[:slots]
+    region_sum_ref[0] = sum_grad[slots:]
+    attended_grad = sum_grad.astype(jnp.bfloat16)
+    add_vector(0, attended_grad.astype(jnp.float32))
+    out_acc[...] += dot_nn(context_ref[0], attended_grad)
+    context_grad_ref[0] = dot_nt(out_weight_ref[...], attended_grad).astype(jnp.bfloat16)
+
+    @pl.when(step == pl.num_programs(0) - 1)
+    def _():
+        out_grad_ref[...] = out_acc[...].astype(jnp.bfloat16)
+        inner_grad_ref[...] = inner_acc[...].astype(jnp.bfloat16)
+        outer_grad_ref[...] = outer_acc[...].astype(jnp.bfloat16)
+
+
+def feed_both(lengths, counts, groups, context, captions, regions, cap_cot, region_cot, square,
+              inner, outer, vectors, inner_bias):
+    seqs, slots, width = captions.shape
+    hidden = inner.shape[1]
+    once = pl.Buffered(1)
+
+    def seq_block(*shape):
+        return pl.BlockSpec((1, *shape), lambda s, *_: (s, 0, 0))
+
+    def whole(shape, column=0):
+        return pl.BlockSpec(shape, lambda s, *_: (0, column), pipeline_mode=once)
+
+    grid_spec = pltpu.PrefetchScalarGridSpec(
+        num_scalar_prefetch=3,
+        grid=(seqs,),
+        in_specs=[
+            seq_block(width, 2 * slots),
+            seq_block(slots, width),
+            pl.BlockSpec((1, slots, width), lambda s, lens, counts, group: (group[s], 0, 0)),
+            seq_block(slots, width),
+            seq_block(slots, width),
+            whole((width, width), 3),
+            whole((width, hidden)),
+            whole((hidden, width)),
+            whole(vectors.shape),
+            whole(inner_bias.shape),
+        ],
+        out_specs=[
+            seq_block(slots, width),
+            seq_block(slots, width),
+            seq_block(slots, width),
+            seq_block(slots, width),
+            seq_block(width, 2 * slots),
+            whole((width, width)),
+            whole((width, hidden)),
+            whole((hidden, width)),
+            whole((8, width)),
+            whole((1, hidden)),
+        ],
+        scratch_shapes=[
+            pltpu.VMEM((2 * slots, hidden), jnp.bfloat16),
+            pltpu.VMEM((2 * slots, hidden), jnp.float32),
+            pltpu.VMEM((width, hidden), jnp.float32),
+            pltpu.VMEM((hidden, width), jnp.float32),
+            pltpu.VMEM((width, width), jnp.float32),
+        ],
+    )
+    low, wide = jnp.bfloat16, jnp.float32
+    rows_shape = (seqs, slots, width)
+    return pl.pallas_call(
+        feed_kernel,
+        grid_spec=grid_spec,
+        out_shape=[
+            jax.ShapeDtypeStruct(rows_shape, low),
+            jax.ShapeDtypeStruct(rows_shape, low),
+            jax.ShapeDtypeStruct(rows_shape, wide),
+            jax.ShapeDtypeStruct(rows_shape, wide),
+            jax.ShapeDtypeStruct((seqs, width, 2 * slots), low),
+            jax.ShapeDtypeStruct((width, width), low),
+            jax.ShapeDtypeStruct((width, hidden), low),
+            jax.ShapeDtypeStruct((hidden, width), low),
+            jax.ShapeDtypeStruct((8, width), wide),
+            jax.ShapeDtypeStruct((1, hidden), wide),
+        ],
+        compiler_params=pltpu.CompilerParams(vmem_limit_bytes=63 * 1024 * 1024),
+        name="feed_both",
+    )(lengths, counts, groups, context, captions, regions, cap_cot, region_cot, square, inner,
+      outer, vectors, inner_bias)
+
+
+def attend_back_kernel(length_ref, count_ref, group_ref, cap_ref, image_ref, lse_ref,
+                       context_grad_ref, rows_ref, image_rows_ref, cap_sum_ref, region_sum_ref,
+                       square_ref, out_grad_ref, cap_grad_out, region_grad_out, square_grad_out,
+                       bias_out, pair_sc, image_acc, region_acc, weight_acc):
+    step = pl.program_id(0)
+    last = pl.num_programs(0) - 1
+    slots, width = rows_ref.shape[1], rows_ref.shape[2]
+    scaling = HEAD ** (-0.5)
+    group = group_ref[step]
+    half = lax.rem(step, 2)
+
+    @pl.when(step == 0)
+    def _():
+        image_acc[...] = jnp.zeros_like(image_acc)
+        region_acc[...] = jnp.zeros_like(region_acc)
+        weight_acc[...] = jnp.zeros_like(weight_acc)
+        bias_out[...] = jnp.zeros_like(bias_out)
+
+    image_part = image_ref.at[group]
+    cap_part = cap_ref.at[0]
+    key_extra = key_mask_rows(length_ref[step], count_ref[step], slots)
+    query_extra = query_mask_rows(slots)
+
+    def heads(turn, carry):
+        for inner in range(HEADS_AT_ONCE):
+            head = turn * HEADS_AT_ONCE + inner
+            query = head_rows(cap_part, image_part, head * HEAD)
+            key = head_rows(cap_part, image_part, width + head * HEAD)
+            value = head_rows(cap_part, image_part, 2 * width + head * HEAD)
+            out_grad = context_grad_ref[0, pl.ds(pl.multiple_of(head * HEAD, HEAD), HEAD), :]
+            scores = dot_tn(
+                jnp.concatenate([key, key_extra], axis=0),
+                jnp.concatenate([query, query_extra], axis=0),
+            )
+            probs = jnp.exp(scores - lse_ref[0, pl.ds(head, 1), :])
+            probs_grad = dot_tn(value, out_grad)
+            value_grad = dot_nt(out_grad, probs.astype(jnp.bfloat16))
+            row_inner = jnp.sum(probs_grad * probs, axis=0, keepdims=True)
+            score_grad = (probs * (probs_grad - row_inner)).astype(jnp.bfloat16)
+            query_grad = dot_nn(key, score_grad) * scaling
+            key_grad = dot_nt(query, score_grad)
+            for part, grad in enumerate((query_grad, key_grad, value_grad)):
+                rows = pl.ds(pl.multiple_of(part * width + head * HEAD, HEAD), HEAD)
+                pair_sc[half, rows, :] = grad[:, :slots].astype(jnp.bfloat16)
+                image_acc[group, rows, :] += grad[:, slots:]
+        return carry
+
+    lax.fori_loop(0, width // HEAD // HEADS_AT_ONCE, heads, 0)
+    region_acc[group] += region_sum_ref[0]
+
+    def flush(first, second, rows):
+        for part in range(3):
+            part_rows = slice(part * width, (part + 1) * width)
+            pair = jnp.concatenate([first[part_rows, :], second[part_rows, :]], axis=1)
+            weight_acc[part_rows, :] += dot_nn(pair, rows)
+            bias_out[part_rows, :] += (
+                first[part_rows, :].astype(jnp.float32) + second[part_rows, :].astype(jnp.float32)
+            )
+            product = dot_nn(square_ref[:, part_rows], pair)
+            turned = product if part == 0 else turned + product
+        return turned.T
+
+    @pl.when(half == 1)
+    def _():
+        rows = rows_ref[...].reshape(2 * slots, width)
+        grad = flush(pair_sc.at[0], pair_sc.at[1], rows)
+        cap_grad_out[...] = cap_sum_ref[...] + grad.reshape(2, slots, width)
+
+    @pl.when(step == last)
+    def _():
+        pair_sc[...] = image_acc[...].astype(jnp.bfloat16)
+        rows = image_rows_ref[...].reshape(2 * slots, width)
+        grad = flush(pair_sc.at[0], pair_sc.at[1], rows)
+        region_grad_out[...] = region_acc[...] + grad.reshape(2, slots, width)
+        square_grad_out[:, : 3 * width] = weight_acc[...].astype(jnp.bfloat16).T
+        square_grad_out[:, 3 * width :] = out_grad_ref[...]
+
+
+def attend_backward(lengths, counts, groups, cap_qkv, image_qkv, lse, context_grad, captions,
+                    regions, cap_sum, region_sum, square, out_grad):
+    seqs, slots, width = captions.shape
+    images = regions.shape[0]
+    heads = width // HEAD
+    once = pl.Buffered(1)
+    all_three = (images, slots, width)
+    grid_spec = pltpu.PrefetchScalarGridSpec(
+        num_scalar_prefetch=3,
+        grid=(seqs,),
+        in_specs=[
+            pl.BlockSpec((1, 3 * width, slots), lambda s, *_: (s, 0, 0)),
+            pl.BlockSpec((images, 3 * width, slots), lambda s, *_: (0, 0, 0), pipeline_mode=once),
+            pl.BlockSpec((1, heads, 2 * slots), lambda s, *_: (s, 0, 0)),
+            pl.BlockSpec((1, width, 2 * slots), lambda s, *_: (s, 0, 0)),
+            pl.BlockSpec((2, slots, width), lambda s, *_: (s // 2, 0, 0)),
+            pl.BlockSpec(all_three, lambda s, *_: (0, 0, 0), pipeline_mode=once),
+            pl.BlockSpec((2, slots, width), lambda s, *_: (s // 2, 0, 0)),
+            pl.BlockSpec((1, slots, width), lambda s, *_: (s, 0, 0)),
+            pl.BlockSpec((width, 3 * width), lambda s, *_: (0, 0), pipeline_mode=once),
+            pl.BlockSpec((width, width), lambda s, *_: (0, 0), pipeline_mode=once),
+        ],
+        out_specs=[
+            pl.BlockSpec((2, slots, width), lambda s, *_: (s // 2, 0, 0)),
+            pl.BlockSpec(all_three, lambda s, *_: (0, 0, 0), pipeline_mode=once),
+            pl.BlockSpec((width, 4 * width), lambda s, *_: (0, 0), pipeline_mode=once),
+            pl.BlockSpec((3 * width, 128), lambda s, *_: (0, 0), pipeline_mode=once),
+        ],
+        scratch_shapes=[
+            pltpu.VMEM((2, 3 * width, slots), jnp.bfloat16),
+            pltpu.VMEM((images, 3 * width, slots), jnp.float32),
+            pltpu.VMEM(all_three, jnp.float32),
+            pltpu.VMEM((3 * width, width), jnp.float32),
+        ],
+    )
+    return pl.pallas_call(
+        attend_back_kernel,
+        grid_spec=grid_spec,
+        out_shape=[
+            jax.ShapeDtypeStruct((seqs, slots, width), jnp.float32),
+            jax.ShapeDtypeStruct(all_three, jnp.float32),
+            jax.ShapeDtypeStruct((width, 4 * width), jnp.bfloat16),
+            jax.ShapeDtypeStruct((3 * width, 128), jnp.float32),
+        ],
+        compiler_params=pltpu.CompilerParams(vmem_limit_bytes=48 * 1024 * 1024),
+        name="attend_backward",
+    )(lengths, counts, groups, cap_qkv, image_qkv, lse, context_grad, captions, regions, cap_sum,
+      region_sum, square, out_grad)
 
 
 def on_device(
@@ -566,18 +982,11 @@
     caption_cotangent,
     region_cotangent,
 ):
-    seq_count = captions.shape[0]
-    caption_slots = captions.shape[1]
-    width_model = captions.shape[2]
-    image_count = regions.shape[0]
-    region_slots = regions.shape[1]
-    row_length = caption_slots + region_slots
-    head_count = HEADS
-    head_size = width_model // head_count
-    scaling = head_size ** (-0.5)
-    all_rows = seq_count * row_length
-    (query_all, key_all, value_all, out_all, inner_all, outer_all), whole_vectors = gather_weights(
-        (query_weight, key_weight, value_weight, out_weight, inner_weight, outer_weight),
+    width = captions.shape[2]
+    square, inner, outer, whole_vectors = gather_weights(
+        (query_weight, key_weight, value_weight, out_weight),
+        inner_weight,
+        outer_weight,
         (
             query_bias,
             value_bias,
@@ -591,204 +1000,87 @@
         ),
         use_kernels,
     )
+    wide = [vector.astype(jnp.float32) for vector in whole_vectors]
+    query_all, value_all, out_all, gain_first, shift_first = wide[:5]
+    inner_all, outer_all, gain_second, shift_second = wide[5:]
+    bias_row = jnp.concatenate([query_all, jnp.zeros_like(query_all), value_all])[None, :]
+    zero_row = jnp.zeros_like(out_all)
+    vectors = jnp.stack(
+        [out_all, gain_first, shift_first, outer_all, gain_second, shift_second, zero_row, zero_row]
+    )
+    seq_counts = jnp.sum(
+        jnp.where(
+            group_ids[:, None] == jnp.arange(regions.shape[0], dtype=jnp.int32)[None, :],
+            region_counts[None, :],
+            0,
+        ),
+        axis=1,
+    )
+    scalars = (caption_lengths, seq_counts, group_ids)
+    cap_qkv, image_qkv, context, lse = attend_forward(
+        *scalars, captions, regions, square, bias_row
+    )
     (
-        query_offset,
-        value_offset,
-        out_offset,
-        gain_first,
-        shift_first,
-        inner_offset,
-        outer_offset,
-        gain_second,
-        shift_second,
-    ) = whole_vectors
-    image_match = group_ids[:, None] == jnp.arange(image_count, dtype=jnp.int32)[None, :]
-    match_low = image_match.astype(jnp.bfloat16)
-    match_float = image_match.astype(jnp.float32)
-    seq_regions = jnp.sum(jnp.where(image_match, region_counts[None, :], 0), axis=1)
-    caption_live = jnp.arange(caption_slots, dtype=jnp.int32)[None, :] < caption_lengths[:, None]
-    region_live = jnp.arange(region_slots, dtype=jnp.int32)[None, :] < seq_regions[:, None]
-    live_rows = jnp.concatenate([caption_live, region_live], axis=1)
-    live_column = live_rows.reshape(all_rows, 1).astype(jnp.float32)
-
-    def spread_images(table):
-        spread_out = jnp.einsum("si,ird->srd", match_low, table, preferred_element_type=jnp.float32)
-        return spread_out.astype(jnp.bfloat16)
-
-    def collect_images(gradient):
-        summed = jnp.einsum("si,srd->ird", match_float, gradient, precision=HIGHEST_PRECISION)
-        return summed.reshape(image_count * region_slots, width_model)
-
-    caption_flat = captions.reshape(seq_count * caption_slots, width_model)
-    region_flat = regions.reshape(image_count * region_slots, width_model)
-
-    def sequence_rows(caption_part, image_part):
-        caption_block = caption_part.reshape(seq_count, caption_slots, width_model)
-        image_block = spread_images(image_part.reshape(image_count, region_slots, width_model))
-        joined = jnp.concatenate([caption_block, image_block], axis=1)
-        return joined.reshape(seq_count, row_length, head_count, head_size)
-
-    def project_three(row_block):
-        query_rows = (forward_rows(row_block, query_all) + query_offset.astype(jnp.float32)).astype(
-            jnp.bfloat16
-        )
-        key_rows = forward_rows(row_block, key_all).astype(jnp.bfloat16)
-        value_rows = (forward_rows(row_block, value_all) + value_offset.astype(jnp.float32)).astype(
-            jnp.bfloat16
-        )
-        return (query_rows, key_rows, value_rows)
-
-    query_caption, key_caption, value_caption = project_three(caption_flat)
-    query_image, key_image, value_image = project_three(region_flat)
-    queries = sequence_rows(query_caption, query_image)
-    keys_seq = sequence_rows(key_caption, key_image)
-    values_seq = sequence_rows(value_caption, value_image)
-
-    def masked_scores():
-        products = (
-            jnp.einsum("sqhe,skhe->shqk", queries, keys_seq, preferred_element_type=jnp.float32)
-            * scaling
-        )
-        return jnp.where(live_rows[:, None, None, :], products, MASKED_SCORE)
-
-    scores = masked_scores()
-    row_max = jnp.max(scores, axis=-1, keepdims=True)
-    log_total = row_max + jnp.log(jnp.sum(jnp.exp(scores - row_max), axis=-1, keepdims=True))
-    probs_low = jnp.exp(scores - log_total).astype(jnp.bfloat16)
-    context = jnp.einsum(
-        "shqk,skhe->sqhe", probs_low, values_seq, preferred_element_type=jnp.float32
-    )
-    context = context.astype(jnp.bfloat16).reshape(all_rows, width_model)
-    inputs_seq = jnp.concatenate([captions, spread_images(regions)], axis=1).reshape(
-        all_rows, width_model
-    )
-    first_sum = (
-        inputs_seq.astype(jnp.float32)
-        + forward_rows(context, out_all)
-        + out_offset.astype(jnp.float32)
-    )
-    first_out, first_back = jax.vjp(
-        normalize, first_sum, gain_first.astype(jnp.float32), shift_first.astype(jnp.float32)
-    )
-    first_low = first_out.astype(jnp.bfloat16)
-    inner_pre = forward_rows(first_low, inner_all) + inner_offset.astype(jnp.float32)
-    active_low = exact_gelu(inner_pre).astype(jnp.bfloat16)
-    second_sum = first_out + forward_rows(active_low, outer_all) + outer_offset.astype(jnp.float32)
-    second_out, second_back = jax.vjp(
-        normalize, second_sum, gain_second.astype(jnp.float32), shift_second.astype(jnp.float32)
-    )
-    layer_out = (second_out * live_column).reshape(seq_count, row_length, width_model)
-    out_caption = layer_out[:, :caption_slots].astype(jnp.bfloat16)
-    out_region = layer_out[:, caption_slots:].astype(jnp.bfloat16)
-    cotangent = jnp.concatenate([caption_cotangent, region_cotangent], axis=1)
-    cotangent = cotangent.reshape(all_rows, width_model).astype(jnp.float32) * live_column
-    second_grad, second_gain_grad, second_shift_grad = second_back(cotangent)
-    inner_back, outer_back = (inner_all, outer_all)
-    outer_grad = second_grad.astype(jnp.bfloat16)
-    outer_weight_grad = weight_grad(active_low, outer_grad)
-    outer_bias_grad = column_sum(outer_grad)
-    active_grad = backward_rows(outer_grad, outer_back)
-    inner_grad = jax.vjp(exact_gelu, inner_pre)[1](active_grad)[0].astype(jnp.bfloat16)
-    inner_weight_grad = weight_grad(first_low, inner_grad)
-    inner_bias_grad = column_sum(inner_grad)
-    first_grad = second_grad + backward_rows(inner_grad, inner_back)
-    sum_grad, first_gain_grad, first_shift_grad = first_back(first_grad)
-    query_back, key_back, value_back, out_back = (query_all, key_all, value_all, out_all)
-    attended_grad = sum_grad.astype(jnp.bfloat16)
-    out_weight_grad = weight_grad(context, attended_grad)
-    out_bias_grad = column_sum(attended_grad)
-    context_grad = backward_rows(attended_grad, out_back).astype(jnp.bfloat16)
-    context_grad = context_grad.reshape(seq_count, row_length, head_count, head_size)
-    scores_again = masked_scores()
-    probs_again = jnp.exp(scores_again - log_total)
-    probs_grad = jnp.einsum(
-        "sqhe,skhe->shqk", context_grad, values_seq, preferred_element_type=jnp.float32
-    )
-    value_grad = jnp.einsum(
-        "shqk,sqhe->skhe",
-        probs_again.astype(jnp.bfloat16),
+        out_caption,
+        out_region,
+        cap_sum,
+        region_sum,
         context_grad,
-        preferred_element_type=jnp.float32,
-    )
-    row_inner = jnp.sum(probs_grad * probs_again, axis=-1, keepdims=True)
-    score_grad = (probs_again * (probs_grad - row_inner)).astype(jnp.bfloat16)
-    query_grad = (
-        jnp.einsum("shqk,skhe->sqhe", score_grad, keys_seq, preferred_element_type=jnp.float32)
-        * scaling
-    )
-    key_grad = (
-        jnp.einsum("shqk,sqhe->skhe", score_grad, queries, preferred_element_type=jnp.float32)
-        * scaling
-    )
-
-    def split_grad(gradient):
-        grid = gradient.reshape(seq_count, row_length, width_model)
-        caption_part = grid[:, :caption_slots].reshape(seq_count * caption_slots, width_model)
-        image_part = collect_images(grid[:, caption_slots:])
-        return (caption_part.astype(jnp.bfloat16), image_part.astype(jnp.bfloat16))
-
-    query_cap_grad, query_img_grad = split_grad(query_grad)
-    key_cap_grad, key_img_grad = split_grad(key_grad)
-    value_cap_grad, value_img_grad = split_grad(value_grad)
-    query_weight_grad = weight_grad(caption_flat, query_cap_grad) + weight_grad(
-        region_flat, query_img_grad
-    )
-    query_bias_grad = column_sum(query_cap_grad) + column_sum(query_img_grad)
-    key_weight_grad = weight_grad(caption_flat, key_cap_grad) + weight_grad(
-        region_flat, key_img_grad
-    )
-    value_weight_grad = weight_grad(caption_flat, value_cap_grad) + weight_grad(
-        region_flat, value_img_grad
-    )
-    value_bias_grad = column_sum(value_cap_grad) + column_sum(value_img_grad)
-    sum_grid = sum_grad.reshape(seq_count, row_length, width_model)
-    caption_input = sum_grid[:, :caption_slots].reshape(seq_count * caption_slots, width_model)
-    caption_input = (
-        caption_input
-        + backward_rows(query_cap_grad, query_back)
-        + backward_rows(key_cap_grad, key_back)
-        + backward_rows(value_cap_grad, value_back)
-    )
-    grad_captions = caption_input.reshape(seq_count, caption_slots, width_model)
-    region_input = (
-        collect_images(sum_grid[:, caption_slots:])
-        + backward_rows(query_img_grad, query_back)
-        + backward_rows(key_img_grad, key_back)
-        + backward_rows(value_img_grad, value_back)
-    )
-    grad_regions = region_input.reshape(image_count, region_slots, width_model)
-    matrix_totals, vector_totals = reduce_weights(
+        out_grad,
+        inner_grad,
+        outer_grad,
+        vector_grads,
+        inner_bias_grad,
+    ) = feed_both(
+        *scalars,
+        context,
+        captions,
+        regions,
+        caption_cotangent,
+        region_cotangent,
+        square,
+        inner,
+        outer,
+        vectors,
+        inner_all[None, :],
+    )
+    grad_captions, grad_regions, square_grad, bias_wide = attend_backward(
+        *scalars,
+        cap_qkv,
+        image_qkv,
+        lse,
+        context_grad,
+        captions,
+        regions,
+        cap_sum,
+        region_sum,
+        square,
+        out_grad,
+    )
+    bias_sums = jnp.sum(bias_wide, axis=1)
+    square_total, inner_total, outer_total, vector_totals = reduce_weights(
+        square_grad,
+        inner_grad,
+        outer_grad,
         (
-            query_weight_grad,
-            key_weight_grad,
-            value_weight_grad,
-            out_weight_grad,
-            inner_weight_grad,
-            outer_weight_grad,
-        ),
-        (
-            query_bias_grad,
-            value_bias_grad,
-            out_bias_grad,
-            first_gain_grad,
-            first_shift_grad,
-            inner_bias_grad,
-            outer_bias_grad,
-            second_gain_grad,
-            second_shift_grad,
+            bias_sums[:width],
+            bias_sums[2 * width :],
+            vector_grads[0],
+            vector_grads[1],
+            vector_grads[2],
+            inner_bias_grad[0],
+            vector_grads[3],
+            vector_grads[4],
+            vector_grads[5],
         ),
         use_kernels,
     )
-    query_total, key_total, value_total, out_total, inner_total, outer_total = matrix_totals
     return (
         out_caption,
         out_region,
         grad_captions,
         grad_regions,
-        query_total,
-        key_total,
-        value_total,
-        out_total,
+        *jnp.split(square_total, 4, axis=1),
         *vector_totals[:5],
         inner_total,
         vector_totals[5],

time: 826 us -> 490 us (0.59); the launches traced: 817 us -> 489 us
  matrix products: 408 us -> 0 us
  Pallas kernels: 190 us -> 465 us
  local copies, waits for them, and re-layouts: 127 us -> 19.3 us
  other arithmetic: 91.2 us -> 4.16 us
    dot_general x41 -> x0, matrix products: 408 us -> none  [the longest x9 132 us: forward_rows(): return jnp.dot(row_block, weight, preferred_element_type=jnp.float32)]
    pallas_call x0 -> x3, Pallas kernels: none -> 275 us  [the longest x1 146 us: feed_both(): pl.pallas_call(feed_kernel, grid_spec=grid_spec, out_shape=[jax.ShapeDtyp...]
    reduce_sum x12 -> x2, other arithmetic: 55.3 us -> 1.13 us  [the longest x1 0.76 us: on_device(): jnp.sum(jnp.where(group_ids[:, None] == jnp.arange(regions.shape[0], dtyp...]
    convert_element_type x2 -> x0, other arithmetic: 27.5 us -> none  [the longest x1 27.5 us: on_device(): score_grad = (probs_again * (probs_grad - row_inner)).astype(jnp.bfloat16)]
    convert_element_type x11 -> x0, local copies, waits for them, and re-layouts: 25.3 us -> none  [the longest x6 10.2 us: split_grad(): return (caption_part.astype(jnp.bfloat16), image_part.astype(jnp.bfloat16))]
    reshape x2 -> x0, local copies, waits for them, and re-layouts: 24.2 us -> none  [on_device(): context_grad.reshape(seq_count, row_length, head_count, head_size)]
    unnamed x102 -> x32, local copies, waits for them, and re-layouts: 28.6 us -> 11.3 us
    concatenate x6 -> x0, local copies, waits for them, and re-layouts: 17.1 us -> none  [sequence_rows(): joined = jnp.concatenate([caption_block, image_block], axis=1)]
where the time goes in v2:
time: 490 us; the launch traced here: 489 us
  Pallas kernels  465 us (95%)
  local copies, waits for them, and re-layouts  19.3 us (4%)
    pallas_call x1, Pallas kernels, feed_both(): pl.pallas_call(feed_kernel, grid_spec=grid_spec, out_shape=[jax.ShapeDtyp...  146 us
    pallas_call x1, Pallas kernels, reduce_all(): pl.pallas_call(functools.partial(reduce_kernel, splits, aligns, owners),...  113 us
    pallas_call x1, Pallas kernels, gather_all(): pl.pallas_call(functools.partial(gather_kernel, splits, aligns), out_shap...  76.2 us
    pallas_call x1, Pallas kernels, attend_backward(): pl.pallas_call(attend_back_kernel, grid_spec=grid_spec, out_shape=[jax.Sh...  70 us
    pallas_call x1, Pallas kernels, attend_forward(): pl.pallas_call(project_kernel, grid_spec=grid_spec, out_shape=[jax.ShapeD...  59.1 us
    unnamed x32, local copies, waits for them, and re-layouts  11.3 us

profile of v2, /device:TPU:0, one launch (start us, length us, event | category | flops | bytes accessed | tf_op | source)
XLA Modules:
  0.0 489.2 jit_solution(11286222566507450601)
XLA Ops:
  0.7 1.7 pad_maximum_fusion.refs_0_
  2.4 0.7 reshape.150
  3.0 0.9 concatenate.14
  3.9 0.6 pad_convert_fusion
  4.5 76.2 %gather_rows.1 = (bf16[768,3072]{1,0:T(8,128)(2,1)}, bf16[768,3072]{1,0:T(8,128)(2,1)}, bf16[3072,768]{1,0:T(8,128)(2,1)}, f32[256,128]{1,0:T(8,128)}) custom-call(bf16[48,3072]{1,0:T(8,128)(2,1)} %pad_maximum_fusion.refs_0_, bf16[48,3072]{1,0:T(8,128)(2,1)} %refs_1_.1, bf16[192,768]{1,0:T(8,128)(2,1)} %refs_2_.1, f32[16,128]{1,0:T(8,128)} %bitcast.29), custom_call_target="tpu_custom_call" | custom-call | tf_op jit(solution)/shard_map/gather_rows/pallas_call | solution.py:211
  80.7 0.9 reshape.156
  81.7 0.1 stack_reshape.18
  82.2 0.6 stack.7.vector_ref
  83.1 0.8 fusion.count_ref
  83.8 1.5 copy-done
  85.4 1.0 copy-done.2
  86.4 0.7 copy-done.7
  87.0 0.7 copy-done.9
  87.7 59.1 %attend_forward.1 = (bf16[10,2304,128]{2,1,0:T(8,128)(2,1)}, bf16[2,2304,128]{2,1,0:T(8,128)(2,1)S(1)}, bf16[10,768,256]{2,1,0:T(8,128)(2,1)}, f32[10,12,256]{2,1,0:T(8,128)S(1)}) custom-call(s32[10]{0:T(128)S(1)} %copy-done.7, s32[10]{0:T(128)S(1)} %fusion.count_ref, s32[10]{0:T(128)S(1)} %copy-done.9, bf16[10,128,768]{2,1,0:T(8,128)(2,1)S(1)} %copy-done, ...), custom_call_target="tpu_custom_call" | custom-call | tf_op jit(solution)/shard_map/attend_forward/pallas_call | solution.py:643
  146.7 1.0 copy-done.4
  147.8 0.7 broadcast_in_dim_reshape.3.inner_bias_ref
  148.5 146.4 %feed_both.1 = (bf16[10,128,768]{2,1,0:T(8,128)(2,1)}, bf16[10,128,768]{2,1,0:T(8,128)(2,1)}, f32[10,128,768]{2,1,0:T(8,128)}, f32[10,128,768]{2,1,0:T(8,128)}, ...) custom-call(s32[10]{0:T(128)} %length_ref.5, ...), custom_call_target="tpu_custom_call" | custom-call | tf_op jit(solution)/shard_map/feed_both/pallas_call | solution.py:811
  295.0 1.5 copy-done.1
  296.5 1.3 copy-done.5
  297.8 1.3 copy-done.6
  299.0 0.7 copy-done.12
  299.7 70.0 %attend_backward.1 = (f32[10,128,768]{2,1,0:T(8,128)}, f32[2,128,768]{2,1,0:T(8,128)}, bf16[768,3072]{1,0:T(8,128)(2,1)}, f32[2304,128]{1,0:T(8,128)S(1)}) custom-call(s32[10]{0:T(128)S(1)} %copy-done.8, s32[10]{0:T(128)S(1)} %copy-done.12, s32[10]{0:T(128)S(1)} %copy-done.10, bf16[10,2304,128]{2,1,0:T(8,128)(2,1)} %get-tuple-element.52.cap_ref, ...), custom_call_target="tpu_custom_call" | custom-call | tf_op jit(solution)/shard_map/attend_backward/pallas_call | solution.py:945
  369.7 0.4 reduce_sum.19
  370.7 0.5 broadcast.15
  371.2 0.7 reduce.15
  372.0 0.1 concatenate.16
  372.2 113.4 %reduce_rows.1 = (f32[48,3072]{1,0:T(8,128)S(1)}, f32[48,3072]{1,0:T(8,128)S(1)}, f32[192,768]{1,0:T(8,128)S(1)}, f32[16,128]{1,0:T(8,128)S(1)}) custom-call(bf16[768,3072]{1,0:T(8,128)(2,1)} %get-tuple-element.61.refs_0_, bf16[768,3072]{1,0:T(8,128)(2,1)} %get-tuple-element.62.refs_1_, bf16[3072,768]{1,0:T(8,128)(2,1)} %get-tuple-element.63.refs_2_, ...), custom_call_target="tpu_custom_call" | custom-call | tf_op jit(solution)/shard_map/reduce_rows/pallas_call | solution.py:425
  485.5 0.8 fusion.1
  486.3 0.6 slice_bitcast_fusion
  486.9 0.6 slice.136
  487.6 0.8 copy.43
  488.4 0.8 copy.44
  (47 shorter events, 1.5 us)
Async XLA Ops:
  83.8 1.5 copy-start
  85.4 1.0 copy-start.2
  86.4 0.7 copy-start.7
  87.0 0.7 copy-start.9
  87.7 60.9 %copy-start.11 = (s32[10]{0:T(128)}, s32[10]{0:T(128)S(1)}, u32[]{:S(2)}) copy-start(s32[10]{0:T(128)S(1)} %fusion.count_ref) | copy-start | bytes 124
  146.7 1.0 copy-start.4
  148.5 146.4 %copy-start.3 = (bf16[2,128,768]{2,1,0:T(8,128)(2,1)S(1)}, bf16[2,128,768]{2,1,0:T(8,128)(2,1)}, u32[]{:S(2)}) copy-start(bf16[2,128,768]{2,1,0:T(8,128)(2,1)} %image_rows_ref.1) | copy-start | bytes 1179652
  148.5 146.4 %copy-start.8 = (s32[10]{0:T(128)S(1)}, s32[10]{0:T(128)}, u32[]{:S(2)}) copy-start(s32[10]{0:T(128)} %length_ref.5) | copy-start | bytes 124
  148.5 146.4 %copy-start.10 = (s32[10]{0:T(128)S(1)}, s32[10]{0:T(128)}, u32[]{:S(2)}) copy-start(s32[10]{0:T(128)} %group_ref.5) | copy-start | bytes 124
  294.9 1.5 copy-start.1
  296.5 1.3 copy-start.5
  297.8 1.3 copy-start.6
  299.0 0.7 copy-start.12
  299.7 70.5 %copy-start.13 = (f32[8,768]{1,0:T(8,128)S(1)}, f32[8,768]{1,0:T(8,128)}, u32[]{:S(2)}) copy-start(f32[8,768]{1,0:T(8,128)} %get-tuple-element.65) | copy-start | bytes 73732
  299.7 71.5 %copy-start.14 = (f32[1,3072]{1,0:T(1,128)S(1)}, f32[1,3072]{1,0:T(1,128)}, u32[]{:S(2)}) copy-start(f32[1,3072]{1,0:T(1,128)} %get-tuple-element.66) | copy-start | bytes 36868

commit v3 on v2

--- a/solution.py
+++ b/solution.py
@@ -46,10 +46,9 @@
     pl.semaphore_wait(barrier, len(peers))
 
 
-def gather_kernel(splits, aligns, *refs):
+def gather_phases(splits, aligns, shards, wholes, sems):
     count = len(splits)
-    shards, wholes = refs[:count], refs[count : 2 * count]
-    (own_sem, z_send, z_recv, a_send, a_recv, b_send, b_recv, s_send, s_recv) = refs[2 * count :]
+    own_sem, z_send, z_recv, a_send, a_recv, b_send, b_recv, s_send, s_recv = sems
     index, half = lax.axis_index("fsdp"), lax.axis_index("rep")
     owners = wholes[0].shape[0] // shards[0].shape[0]
 
@@ -70,33 +69,67 @@
             device_id_type=MESH,
         )
 
+    def source_of(tensor, step, first, second):
+        if step + first + second == 0:
+            return part_of(shards[tensor], splits[tensor], 0, half, 1, aligns[tensor])
+        return piece(tensor, step, first, second)
+
     peer_a = (owner_of(0, 1, 0), half)
     peer_b = (owner_of(0, 0, 1), half)
     sibling = (index, 1 - half)
 
-    def to_z(tensor, source, hop):
+    def to_z(tensor, hop):
         peer = (owner_of(hop, 0, 0), half)
         slot = PLANES - hop - 1
+        source = source_of(tensor, 0, 0, 0)
         return copy_piece(
             tensor, source, 0, 0, 0, z_send.at[tensor, hop - 1], z_recv.at[tensor, slot], peer
         )
 
-    def to_a(tensor, source, step):
+    def from_z(tensor, step):
+        source = piece(tensor, step, 0, 0)
+        return copy_piece(
+            tensor,
+            source,
+            step,
+            0,
+            0,
+            z_send.at[tensor, step - 1],
+            z_recv.at[tensor, step - 1],
+            sibling,
+        )
+
+    def to_a(tensor, step):
+        source = source_of(tensor, step, 0, 0)
         return copy_piece(
             tensor, source, step, 0, 0, a_send.at[tensor, step], a_recv.at[tensor, step], peer_a
         )
 
-    def to_b(tensor, source, step, first):
+    def from_a(tensor, step):
+        source = piece(tensor, step, 1, 0)
+        return copy_piece(
+            tensor, source, step, 1, 0, a_send.at[tensor, step], a_recv.at[tensor, step], peer_a
+        )
+
+    def to_b(tensor, step, first):
         slot = step * 2 + first
+        source = source_of(tensor, step, first, 0)
         return copy_piece(
             tensor, source, step, first, 0, b_send.at[tensor, slot], b_recv.at[tensor, slot], peer_b
         )
 
-    def to_sibling(tensor, source, step, first, second):
+    def from_b(tensor, step, first):
+        slot = step * 2 + first
+        source = piece(tensor, step, first, 1)
+        return copy_piece(
+            tensor, source, step, first, 1, b_send.at[tensor, slot], b_recv.at[tensor, slot], peer_b
+        )
+
+    def to_sibling(tensor, step, first, second):
         slot = step * 4 + first * 2 + second - 1
         return copy_piece(
             tensor,
-            source,
+            piece(tensor, step, first, second),
             step,
             first,
             second,
@@ -105,143 +138,126 @@
             sibling,
         )
 
-    greet(index, half)
-    started = []
-    local = []
-    for tensor in range(count):
-        shard = shards[tensor]
-        rows = shard.shape[0]
-        source = part_of(shard, splits[tensor], 0, half, 1, aligns[tensor])
-        sends = [to_z(tensor, source, hop) for hop in (1, 2, 3)]
-        sends += [to_a(tensor, source, 0), to_b(tensor, source, 0, 0)]
-        for copy in sends:
-            copy.start()
-        started += sends
-        here = pltpu.make_async_copy(
-            shard,
-            wholes[tensor].at[pl.ds(pl.multiple_of(index * rows, aligns[tensor]), rows)],
-            own_sem.at[tensor],
-        )
-        here.start()
-        local.append(here)
-    for tensor in range(count):
-        for step in (1, 2, 3):
-            source = piece(tensor, step, 0, 0)
-            copy_piece(
-                tensor,
-                source,
-                step,
-                0,
-                0,
-                z_send.at[tensor, step - 1],
-                z_recv.at[tensor, step - 1],
-                sibling,
-            ).wait_recv()
-            sends = [
-                to_b(tensor, source, step, 0),
-                to_a(tensor, source, step),
-                to_sibling(tensor, source, step, 0, 0),
-            ]
-            for copy in sends:
-                copy.start()
-            started += sends
-    for tensor in range(count):
-        for step in range(PLANES):
-            source = piece(tensor, step, 1, 0)
-            copy_piece(
-                tensor,
-                source,
-                step,
-                1,
-                0,
-                a_send.at[tensor, step],
-                a_recv.at[tensor, step],
-                peer_a,
-            ).wait_recv()
-            sends = [to_b(tensor, source, step, 1), to_sibling(tensor, source, step, 1, 0)]
-            for copy in sends:
-                copy.start()
-            started += sends
-    for tensor in range(count):
-        for step in range(PLANES):
-            for first in (0, 1):
-                source = piece(tensor, step, first, 1)
-                slot = step * 2 + first
-                copy_piece(
-                    tensor,
-                    source,
-                    step,
-                    first,
-                    1,
-                    b_send.at[tensor, slot],
-                    b_recv.at[tensor, slot],
-                    peer_b,
-                ).wait_recv()
-                copy = to_sibling(tensor, source, step, first, 1)
-                copy.start()
-                started.append(copy)
-    for tensor in range(count):
-        local[tensor].wait()
-        for step in range(PLANES):
-            for first in (0, 1):
-                for second in (0, 1):
-                    if step + first + second == 0:
-                        continue
-                    slot = step * 4 + first * 2 + second - 1
-                    owner = place_of(index, 1 - half, step, first, second)
-                    there = part_of(
-                        wholes[tensor], splits[tensor], owner, 1 - half, owners, aligns[tensor]
-                    )
-                    pltpu.make_async_remote_copy(
-                        src_ref=there,
-                        dst_ref=there,
-                        send_sem=s_send.at[tensor, slot],
-                        recv_sem=s_recv.at[tensor, slot],
-                        device_id=sibling,
-                        device_id_type=MESH,
-                    ).wait_recv()
-    for copy in started:
-        copy.wait_send()
+    def from_sibling(tensor, step, first, second):
+        slot = step * 4 + first * 2 + second - 1
+        owner = place_of(index, 1 - half, step, first, second)
+        there = part_of(wholes[tensor], splits[tensor], owner, 1 - half, owners, aligns[tensor])
+        return pltpu.make_async_remote_copy(
+            src_ref=there,
+            dst_ref=there,
+            send_sem=s_send.at[tensor, slot],
+            recv_sem=s_recv.at[tensor, slot],
+            device_id=sibling,
+            device_id_type=MESH,
+        )
+
+    def own(tensor):
+        rows = shards[tensor].shape[0]
+        start = pl.multiple_of(index * rows, aligns[tensor])
+        return pltpu.make_async_copy(
+            shards[tensor], wholes[tensor].at[pl.ds(start, rows)], own_sem.at[tensor]
+        )
+
+    def start():
+        greet(index, half)
+        for tensor in range(count):
+            for hop in (1, 2, 3):
+                to_z(tensor, hop).start()
+            to_a(tensor, 0).start()
+            to_b(tensor, 0, 0).start()
+            own(tensor).start()
+
+    def pass_z(tensor, steps=(1, 2, 3)):
+        for step in steps:
+            from_z(tensor, step).wait_recv()
+            to_b(tensor, step, 0).start()
+            to_a(tensor, step).start()
+            to_sibling(tensor, step, 0, 0).start()
+
+    def pass_a(tensor, steps=(0, 1, 2, 3)):
+        for step in steps:
+            from_a(tensor, step).wait_recv()
+            to_b(tensor, step, 1).start()
+            to_sibling(tensor, step, 1, 0).start()
+
+    def pass_b(tensor, steps=(0, 1, 2, 3), firsts=(0, 1)):
+        for step in steps:
+            for first in firsts:
+                from_b(tensor, step, first).wait_recv()
+                to_sibling(tensor, step, first, 1).start()
+
+    def finish():
+        for tensor in range(count):
+            own(tensor).wait()
+            for step in range(PLANES):
+                for first in (0, 1):
+                    for second in (0, 1):
+                        if step + first + second == 0:
+                            continue
+                        from_sibling(tensor, step, first, second).wait_recv()
+                        to_sibling(tensor, step, first, second).wait_send()
+                    to_b(tensor, step, first).wait_send()
+                to_a(tensor, step).wait_send()
+                if step > 0:
+                    to_z(tensor, step).wait_send()
+
+    return start, pass_z, pass_a, pass_b, finish
+
+
+def gather_kernel(splits, aligns, *refs):
+    count = len(splits)
+    start, pass_z, pass_a, pass_b, finish = gather_phases(
+        splits, aligns, refs[:count], refs[count : 2 * count], refs[2 * count :]
+    )
+    start()
+    for move in (pass_z, pass_a, pass_b):
+        for tensor in range(count):
+            move(tensor)
+    finish()
+
+
+def gather_semaphores(count):
+    dma = pltpu.SemaphoreType.DMA
+    return [
+        dma((count,)),
+        dma((count, 3)),
+        dma((count, 3)),
+        dma((count, 4)),
+        dma((count, 4)),
+        dma((count, 8)),
+        dma((count, 8)),
+        dma((count, 15)),
+        dma((count, 15)),
+    ]
+
+
+def tile_rows(arrays):
+    return [16 if array.dtype == jnp.bfloat16 else 8 for array in arrays]
 
 
 def gather_all(shards, splits, owners, collective_id):
     count = len(shards)
-    aligns = [16 if shard.dtype == jnp.bfloat16 else 8 for shard in shards]
-    dma = pltpu.SemaphoreType.DMA
     return pl.pallas_call(
-        functools.partial(gather_kernel, splits, aligns),
+        functools.partial(gather_kernel, splits, tile_rows(shards)),
         out_shape=[
             jax.ShapeDtypeStruct((owners * shard.shape[0], shard.shape[1]), shard.dtype)
             for shard in shards
         ],
         in_specs=[pl.BlockSpec(memory_space=pltpu.VMEM)] * count,
         out_specs=[pl.BlockSpec(memory_space=pl.ANY)] * count,
-        scratch_shapes=[
-            dma((count,)),
-            dma((count, 3)),
-            dma((count, 3)),
-            dma((count, 4)),
-            dma((count, 4)),
-            dma((count, 8)),
-            dma((count, 8)),
-            dma((count, 15)),
-            dma((count, 15)),
-        ],
+        scratch_shapes=gather_semaphores(count),
         compiler_params=pltpu.CompilerParams(collective_id=collective_id, has_side_effects=True),
         name="gather_rows",
     )(*shards)
 
 
-def reduce_kernel(splits, aligns, owners, *refs):
+def reduce_phases(splits, aligns, owners, partials, totals, buffers, sems):
     count = len(splits)
-    partials, totals = refs[:count], refs[count : 2 * count]
-    mine = refs[2 * count : 3 * count]
-    core_in = refs[3 * count : 4 * count]
-    b_in = refs[4 * count : 5 * count]
-    a_in = refs[5 * count : 6 * count]
-    z_in = refs[6 * count : 7 * count]
+    mine, core_in, b_in, a_in, z_in = [
+        buffers[kind * count : (kind + 1) * count] for kind in range(5)
+    ]
     (load_sem, c_send, c_recv, b_send, b_recv, a_send, a_recv, z_send, z_recv, o_send, o_recv) = (
-        refs[7 * count :]
+        sems
     )
     index, half = lax.axis_index("fsdp"), lax.axis_index("rep")
     sibling = (index, 1 - half)
@@ -321,18 +337,40 @@
             device_id_type=MESH,
         )
 
-    greet(index, half)
+    def from_z(tensor, hop):
+        slot = PLANES - hop - 1
+        return pltpu.make_async_remote_copy(
+            src_ref=mine[tensor].at[hop],
+            dst_ref=z_in[tensor].at[slot],
+            send_sem=z_send.at[tensor, hop - 1],
+            recv_sem=z_recv.at[tensor, slot],
+            device_id=sibling,
+            device_id_type=MESH,
+        )
+
+    def from_output(tensor):
+        there = part_of(totals[tensor], splits[tensor], 0, 1 - half, 1, 8)
+        return pltpu.make_async_remote_copy(
+            src_ref=there,
+            dst_ref=there,
+            send_sem=o_send.at[tensor],
+            recv_sem=o_recv.at[tensor],
+            device_id=sibling,
+            device_id_type=MESH,
+        )
 
     order = [(step, first, 1) for first in (1, 0) for step in (1, 2, 3, 0)]
     order += [(step, 1, 0) for step in (1, 2, 3, 0)] + [(step, 0, 0) for step in (1, 2, 3, 0)]
-    for tensor in range(count):
-        for step, first, second in order:
-            to_core(tensor, step, first, second).start()
-            load(tensor, step, first, second).start()
-
-    for tensor in range(count):
-
-        def b_step(turn, carry, tensor=tensor):
+
+    def start():
+        greet(index, half)
+        for tensor in range(count):
+            for step, first, second in order:
+                to_core(tensor, step, first, second).start()
+                load(tensor, step, first, second).start()
+
+    def send_b(tensor):
+        def turn_b(turn, carry):
             step, first = lax.rem(turn + 1, PLANES), 1 - turn // PLANES
             load(tensor, step, first, 1).wait()
             to_core(tensor, step, first, 1).wait_recv()
@@ -342,10 +380,10 @@
             to_b(tensor, step, first).start()
             return carry
 
-        lax.fori_loop(0, 2 * PLANES, b_step, 0)
-    for tensor in range(count):
-
-        def a_step(turn, carry, tensor=tensor):
+        lax.fori_loop(0, 2 * PLANES, turn_b, 0)
+
+    def send_a(tensor):
+        def turn_a(turn, carry):
             step = lax.rem(turn + 1, PLANES)
             load(tensor, step, 1, 0).wait()
             to_core(tensor, step, 1, 0).wait_recv()
@@ -357,10 +395,10 @@
             to_a(tensor, step).start()
             return carry
 
-        lax.fori_loop(0, PLANES, a_step, 0)
-    for tensor in range(count):
-
-        def total_of(step, tensor=tensor):
+        lax.fori_loop(0, PLANES, turn_a, 0)
+
+    def send_z(tensor):
+        def total_of(step):
             load(tensor, step, 0, 0).wait()
             to_core(tensor, step, 0, 0).wait_recv()
             to_b(tensor, step, 0).wait_recv()
@@ -373,45 +411,52 @@
             to_z(tensor, hop).start()
         mine_total = total_of(0)
         output_part(tensor)[...] = mine_total
-    for tensor in range(count):
+
+    def send_output(tensor):
         out = output_part(tensor)
         total = out[...]
         for hop in (1, 2, 3):
-            slot = PLANES - hop - 1
-            pltpu.make_async_remote_copy(
-                src_ref=mine[tensor].at[hop],
-                dst_ref=z_in[tensor].at[slot],
-                send_sem=z_send.at[tensor, hop - 1],
-                recv_sem=z_recv.at[tensor, slot],
-                device_id=sibling,
-                device_id_type=MESH,
-            ).wait_recv()
-            total += wide(z_in[tensor].at[slot])
+            from_z(tensor, hop).wait_recv()
+            total += wide(z_in[tensor].at[PLANES - hop - 1])
         out[...] = total
         to_output(tensor).start()
-    for tensor in range(count):
-        pltpu.make_async_remote_copy(
-            src_ref=part_of(totals[tensor], splits[tensor], 0, 1 - half, 1, 8),
-            dst_ref=part_of(totals[tensor], splits[tensor], 0, 1 - half, 1, 8),
-            send_sem=o_send.at[tensor],
-            recv_sem=o_recv.at[tensor],
-            device_id=sibling,
-            device_id_type=MESH,
-        ).wait_recv()
-        to_output(tensor).wait_send()
-        for step, first, second in order:
-            to_core(tensor, step, first, second).wait_send()
-            if second == 1:
-                to_b(tensor, step, first).wait_send()
-            elif first == 1:
-                to_a(tensor, step).wait_send()
-            elif step > 0:
-                to_z(tensor, step).wait_send()
-
-
-def reduce_all(partials, splits, owners, collective_id):
+
+    def finish():
+        for tensor in range(count):
+            from_output(tensor).wait_recv()
+            to_output(tensor).wait_send()
+            for step, first, second in order:
+                to_core(tensor, step, first, second).wait_send()
+                if second == 1:
+                    to_b(tensor, step, first).wait_send()
+                elif first == 1:
+                    to_a(tensor, step).wait_send()
+                elif step > 0:
+                    to_z(tensor, step).wait_send()
+
+    return start, send_b, send_a, send_z, send_output, finish
+
+
+def reduce_kernel(splits, aligns, owners, *refs):
+    count = len(splits)
+    start, *moves, finish = reduce_phases(
+        splits,
+        aligns,
+        owners,
+        refs[:count],
+        refs[count : 2 * count],
+        refs[2 * count : 7 * count],
+        refs[7 * count :],
+    )
+    start()
+    for move in moves:
+        for tensor in range(count):
+            move(tensor)
+    finish()
+
+
+def reduce_scratch(partials, splits, owners):
     count = len(partials)
-    aligns = [16 if part.dtype == jnp.bfloat16 else 8 for part in partials]
     dma = pltpu.SemaphoreType.DMA
 
     def pieces(slots):
@@ -422,32 +467,35 @@
             shapes.append(pltpu.VMEM((slots, *shape), part.dtype))
         return shapes
 
+    buffers = [*pieces(16), *pieces(16), *pieces(8), *pieces(4), *pieces(3)]
+    sems = [
+        dma((count, 16)),
+        dma((count, 16)),
+        dma((count, 16)),
+        dma((count, 8)),
+        dma((count, 8)),
+        dma((count, 4)),
+        dma((count, 4)),
+        dma((count, 3)),
+        dma((count, 3)),
+        dma((count,)),
+        dma((count,)),
+    ]
+    return buffers, sems
+
+
+def reduce_all(partials, splits, owners, collective_id):
+    count = len(partials)
+    buffers, sems = reduce_scratch(partials, splits, owners)
     return pl.pallas_call(
-        functools.partial(reduce_kernel, splits, aligns, owners),
+        functools.partial(reduce_kernel, splits, tile_rows(partials), owners),
         out_shape=[
             jax.ShapeDtypeStruct((part.shape[0] // owners, part.shape[1]), jnp.float32)
             for part in partials
         ],
         in_specs=[pl.BlockSpec(memory_space=pl.ANY)] * count,
         out_specs=[pl.BlockSpec(memory_space=pltpu.VMEM)] * count,
-        scratch_shapes=[
-            *pieces(16),
-            *pieces(16),
-            *pieces(8),
-            *pieces(4),
-            *pieces(3),
-            dma((count, 16)),
-            dma((count, 16)),
-            dma((count, 16)),
-            dma((count, 8)),
-            dma((count, 8)),
-            dma((count, 4)),
-            dma((count, 4)),
-            dma((count, 3)),
-            dma((count, 3)),
-            dma((count,)),
-            dma((count,)),
-        ],
+        scratch_shapes=[*buffers, *sems],
         compiler_params=pltpu.CompilerParams(
             collective_id=collective_id, has_side_effects=True, vmem_limit_bytes=48 * 1024 * 1024
         ),
@@ -457,7 +505,8 @@
 
 OWNERS = 16
 VECTOR_ROWS = 16
-WEIGHT_SPLITS = (COLUMN_SPLIT, COLUMN_SPLIT, ROW_SPLIT, ROW_SPLIT)
+SQUARE_SPLITS = (COLUMN_SPLIT, ROW_SPLIT)
+FEED_SPLITS = (COLUMN_SPLIT, ROW_SPLIT)
 
 
 def pack_vectors(parts, owners):
@@ -475,32 +524,27 @@
     return vectors
 
 
-def gather_weights(squares, inner, outer, vectors, use_kernels):
+def gather_weights(squares, vectors, use_kernels):
     square = jnp.concatenate(squares, axis=1)
     if not use_kernels:
-        whole = [lax.all_gather(m, "fsdp", axis=0, tiled=True) for m in (square, inner, outer)]
-        return *whole, [lax.all_gather(v, "fsdp", axis=0, tiled=True) for v in vectors]
+        whole = [lax.all_gather(part, "fsdp", axis=0, tiled=True) for part in (square, *vectors)]
+        return whole[0], whole[1:]
     packed = pack_vectors(vectors, 1)
-    square, inner, outer, packed = gather_all(
-        (square, inner, outer, packed), WEIGHT_SPLITS, OWNERS, 1
-    )
-    return square, inner, outer, unpack_vectors(packed, OWNERS, [v.shape[0] for v in vectors])
-
-
-def reduce_weights(square, inner, outer, vectors, use_kernels):
+    square, packed = gather_all((square, packed), SQUARE_SPLITS, OWNERS, 1)
+    return square, unpack_vectors(packed, OWNERS, [v.shape[0] for v in vectors])
+
+
+def reduce_native(part):
+    share = lax.psum_scatter(part.astype(jnp.float32), "fsdp", scatter_dimension=0, tiled=True)
+    return lax.psum(share.astype(jnp.bfloat16), "rep").astype(jnp.float32)
+
+
+def reduce_weights(square, vectors, use_kernels):
     if not use_kernels:
-        totals = []
-        for part in (square, inner, outer, *vectors):
-            wide = part.astype(jnp.float32)
-            share = lax.psum_scatter(wide, "fsdp", scatter_dimension=0, tiled=True)
-            totals.append(lax.psum(share.astype(jnp.bfloat16), "rep").astype(jnp.float32))
-        return *totals[:3], totals[3:]
+        return reduce_native(square), [reduce_native(vector) for vector in vectors]
     packed = pack_vectors(vectors, OWNERS)
-    square, inner, outer, packed = reduce_all(
-        (square, inner, outer, packed), WEIGHT_SPLITS, OWNERS, 2
-    )
-    sizes = [v.shape[0] // OWNERS for v in vectors]
-    return square, inner, outer, unpack_vectors(packed, 1, sizes)
+    square, packed = reduce_all((square, packed), SQUARE_SPLITS, OWNERS, 2)
+    return square, unpack_vectors(packed, 1, [v.shape[0] // OWNERS for v in vectors])
 
 
 def dot_nn(left, right):
@@ -549,9 +593,49 @@
     return jnp.concatenate([cap_part[rows, :], image_part[rows, :]], axis=1)
 
 
-def project_kernel(length_ref, count_ref, group_ref, cap_ref, image_ref, weight_ref, bias_ref,
-                   cap_out, image_out, context_out, lse_out, weight_turned, bias_wide):
+def project_kernel(share, length_ref, count_ref, group_ref, cap_ref, image_ref, weight_ref,
+                   bias_ref, *refs):
+    shards, refs = refs[:share], refs[share:]
+    (cap_out, image_out, context_out, lse_out), refs = refs[:4], refs[4:]
+    wholes, refs = refs[:share], refs[share:]
+    (weight_turned, bias_wide), sems = refs[:2], refs[2:]
     step = pl.program_id(0)
+    if share:
+        start, pass_z, pass_a, pass_b, finish = gather_phases(
+            FEED_SPLITS, tile_rows(shards), shards, wholes, sems
+        )
+        later = (1, 2, 3)
+
+        @pl.when(step == 0)
+        def _():
+            start()
+
+        @pl.when(step == 1)
+        def _():
+            pass_a(0, (0,))
+            pass_a(1, (0,))
+            pass_z(0)
+
+        @pl.when(step == 2)
+        def _():
+            pass_a(0, later)
+
+        @pl.when(step == 3)
+        def _():
+            pass_z(1)
+            pass_b(0, (0,))
+
+        @pl.when(step == 4)
+        def _():
+            pass_a(1, later)
+            pass_b(1, (0,))
+
+        for turn, (tensor, first) in enumerate(((0, 0), (0, 1), (1, 0), (1, 1))):
+
+            @pl.when(step == 5 + turn)
+            def _(tensor=tensor, first=first):
+                pass_b(tensor, later, (first,))
+
     width = cap_ref.shape[2]
     slots = cap_ref.shape[1]
     scaling = HEAD ** (-0.5)
@@ -614,44 +698,60 @@
         return carry
 
     lax.fori_loop(0, width // HEAD // HEADS_AT_ONCE, heads, 0)
-
-
-def attend_forward(lengths, counts, groups, captions, regions, square, bias_row):
+    if share:
+
+        @pl.when(step == pl.num_programs(0) - 1)
+        def _():
+            finish()
+
+
+SCALARS = [pl.BlockSpec(memory_space=pltpu.SMEM)] * 3
+
+
+def attend_forward(lengths, counts, groups, captions, regions, square, bias_row, shards):
     seqs, slots, width = captions.shape
     images = regions.shape[0]
     heads = width // HEAD
-    grid_spec = pltpu.PrefetchScalarGridSpec(
-        num_scalar_prefetch=3,
+    share = len(shards)
+    params = {"collective_id": 3, "has_side_effects": True} if share else {}
+    low, wide = jnp.bfloat16, jnp.float32
+    anywhere = [pl.BlockSpec(memory_space=pl.ANY)] * share
+    return pl.pallas_call(
+        functools.partial(project_kernel, share),
         grid=(seqs,),
         in_specs=[
-            pl.BlockSpec((2, slots, width), lambda s, *_: (s // 2, 0, 0)),
-            pl.BlockSpec((images, slots, width), lambda s, *_: (0, 0, 0)),
-            pl.BlockSpec(square.shape, lambda s, *_: (0, 0), pipeline_mode=pl.Buffered(1)),
-            pl.BlockSpec(bias_row.shape, lambda s, *_: (0, 0)),
+            *SCALARS,
+            pl.BlockSpec((2, slots, width), lambda s: (s // 2, 0, 0)),
+            pl.BlockSpec((images, slots, width), lambda s: (0, 0, 0)),
+            pl.BlockSpec(square.shape, lambda s: (0, 0), pipeline_mode=pl.Buffered(1)),
+            pl.BlockSpec(bias_row.shape, lambda s: (0, 0)),
+            *anywhere,
         ],
         out_specs=[
-            pl.BlockSpec((2, 3 * width, slots), lambda s, *_: (s // 2, 0, 0)),
-            pl.BlockSpec((images, 3 * width, slots), lambda s, *_: (0, 0, 0)),
-            pl.BlockSpec((1, width, 2 * slots), lambda s, *_: (s, 0, 0)),
-            pl.BlockSpec((1, heads, 2 * slots), lambda s, *_: (s, 0, 0)),
+            pl.BlockSpec((2, 3 * width, slots), lambda s: (s // 2, 0, 0)),
+            pl.BlockSpec((images, 3 * width, slots), lambda s: (0, 0, 0)),
+            pl.BlockSpec((1, width, 2 * slots), lambda s: (s, 0, 0)),
+            pl.BlockSpec((1, heads, 2 * slots), lambda s: (s, 0, 0)),
+            *anywhere,
         ],
         scratch_shapes=[
-            pltpu.VMEM((3 * width, width), jnp.bfloat16),
-            pltpu.VMEM((3 * width, 128), jnp.float32),
-        ],
-    )
-    return pl.pallas_call(
-        project_kernel,
-        grid_spec=grid_spec,
+            pltpu.VMEM((3 * width, width), low),
+            pltpu.VMEM((3 * width, 128), wide),
+            *(gather_semaphores(share) if share else ()),
+        ],
         out_shape=[
-            jax.ShapeDtypeStruct((seqs, 3 * width, slots), jnp.bfloat16),
-            jax.ShapeDtypeStruct((images, 3 * width, slots), jnp.bfloat16),
-            jax.ShapeDtypeStruct((seqs, width, 2 * slots), jnp.bfloat16),
-            jax.ShapeDtypeStruct((seqs, heads, 2 * slots), jnp.float32),
-        ],
-        compiler_params=pltpu.CompilerParams(vmem_limit_bytes=48 * 1024 * 1024),
+            jax.ShapeDtypeStruct((seqs, 3 * width, slots), low),
+            jax.ShapeDtypeStruct((images, 3 * width, slots), low),
+            jax.ShapeDtypeStruct((seqs, width, 2 * slots), low),
+            jax.ShapeDtypeStruct((seqs, heads, 2 * slots), wide),
+            *[
+                jax.ShapeDtypeStruct((OWNERS * shard.shape[0], shard.shape[1]), shard.dtype)
+                for shard in shards
+            ],
+        ],
+        compiler_params=pltpu.CompilerParams(vmem_limit_bytes=48 * 1024 * 1024, **params),
         name="attend_forward",
-    )(lengths, counts, groups, captions, regions, square, bias_row)
+    )(lengths, counts, groups, captions, regions, square, bias_row, *shards)
 
 
 PHI_SLOPE = 0.2316419
@@ -829,12 +929,34 @@
       outer, vectors, inner_bias)
 
 
-def attend_back_kernel(length_ref, count_ref, group_ref, cap_ref, image_ref, lse_ref,
+def attend_back_kernel(share, length_ref, count_ref, group_ref, cap_ref, image_ref, lse_ref,
                        context_grad_ref, rows_ref, image_rows_ref, cap_sum_ref, region_sum_ref,
-                       square_ref, out_grad_ref, cap_grad_out, region_grad_out, square_grad_out,
-                       bias_out, pair_sc, image_acc, region_acc, weight_acc):
+                       square_ref, out_grad_ref, *refs):
+    partials, refs = refs[:share], refs[share:]
+    (cap_grad_out, region_grad_out, square_grad_out, bias_out), refs = refs[:4], refs[4:]
+    total_outs, refs = refs[:share], refs[share:]
+    (pair_sc, image_acc, region_acc, weight_acc), refs = refs[:4], refs[4:]
+    totals, buffers, sems = refs[:share], refs[share : 6 * share], refs[6 * share :]
     step = pl.program_id(0)
     last = pl.num_programs(0) - 1
+    images = image_ref.shape[0]
+    if share:
+        start, send_b, send_a, send_z, send_output, finish = reduce_phases(
+            FEED_SPLITS, tile_rows(partials), OWNERS, partials, totals, buffers, sems
+        )
+
+        @pl.when(step == 0)
+        def _():
+            start()
+
+        schedule = ((1, send_b, 0), (2, send_b, 1), (4, send_a, 0), (5, send_a, 1))
+        schedule += ((6, send_z, 0), (7, send_z, 1), (8, send_output, 0))
+        for when, move, tensor in schedule:
+
+            @pl.when(step == when)
+            def _(move=move, tensor=tensor):
+                move(tensor)
+
     slots, width = rows_ref.shape[1], rows_ref.shape[2]
     scaling = HEAD ** (-0.5)
     group = group_ref[step]
@@ -848,6 +970,7 @@
         bias_out[...] = jnp.zeros_like(bias_out)
 
     image_part = image_ref.at[group]
+    uses = [(group == image).astype(jnp.float32) for image in range(images)]
     cap_part = cap_ref.at[0]
     key_extra = key_mask_rows(length_ref[step], count_ref[step], slots)
     query_extra = query_mask_rows(slots)
@@ -873,11 +996,13 @@
             for part, grad in enumerate((query_grad, key_grad, value_grad)):
                 rows = pl.ds(pl.multiple_of(part * width + head * HEAD, HEAD), HEAD)
                 pair_sc[half, rows, :] = grad[:, :slots].astype(jnp.bfloat16)
-                image_acc[group, rows, :] += grad[:, slots:]
+                for image in range(images):
+                    image_acc[image, rows, :] += grad[:, slots:] * uses[image]
         return carry
 
     lax.fori_loop(0, width // HEAD // HEADS_AT_ONCE, heads, 0)
-    region_acc[group] += region_sum_ref[0]
+    for image in range(images):
+        region_acc[image] += region_sum_ref[0] * uses[image]
 
     def flush(first, second, rows):
         for part in range(3):
@@ -905,56 +1030,73 @@
         region_grad_out[...] = region_acc[...] + grad.reshape(2, slots, width)
         square_grad_out[:, : 3 * width] = weight_acc[...].astype(jnp.bfloat16).T
         square_grad_out[:, 3 * width :] = out_grad_ref[...]
+        if share:
+            send_output(1)
+            finish()
+            for out, total in zip(total_outs, totals):
+                out[...] = total[...]
 
 
 def attend_backward(lengths, counts, groups, cap_qkv, image_qkv, lse, context_grad, captions,
-                    regions, cap_sum, region_sum, square, out_grad):
+                    regions, cap_sum, region_sum, square, out_grad, partials):
     seqs, slots, width = captions.shape
     images = regions.shape[0]
     heads = width // HEAD
+    share = len(partials)
+    params = {"collective_id": 4, "has_side_effects": True} if share else {}
     once = pl.Buffered(1)
+    low, wide = jnp.bfloat16, jnp.float32
     all_three = (images, slots, width)
-    grid_spec = pltpu.PrefetchScalarGridSpec(
-        num_scalar_prefetch=3,
+    shapes = [(part.shape[0] // OWNERS, part.shape[1]) for part in partials]
+    buffers, sems = reduce_scratch(partials, FEED_SPLITS, OWNERS) if share else ((), ())
+
+    def whole(*shape):
+        return pl.BlockSpec(shape, lambda s: (0,) * len(shape), pipeline_mode=once)
+
+    return pl.pallas_call(
+        functools.partial(attend_back_kernel, share),
         grid=(seqs,),
         in_specs=[
-            pl.BlockSpec((1, 3 * width, slots), lambda s, *_: (s, 0, 0)),
-            pl.BlockSpec((images, 3 * width, slots), lambda s, *_: (0, 0, 0), pipeline_mode=once),
-            pl.BlockSpec((1, heads, 2 * slots), lambda s, *_: (s, 0, 0)),
-            pl.BlockSpec((1, width, 2 * slots), lambda s, *_: (s, 0, 0)),
-            pl.BlockSpec((2, slots, width), lambda s, *_: (s // 2, 0, 0)),
-            pl.BlockSpec(all_three, lambda s, *_: (0, 0, 0), pipeline_mode=once),
-            pl.BlockSpec((2, slots, width), lambda s, *_: (s // 2, 0, 0)),
-            pl.BlockSpec((1, slots, width), lambda s, *_: (s, 0, 0)),
-            pl.BlockSpec((width, 3 * width), lambda s, *_: (0, 0), pipeline_mode=once),
-            pl.BlockSpec((width, width), lambda s, *_: (0, 0), pipeline_mode=once),
+            *SCALARS,
+            pl.BlockSpec((1, 3 * width, slots), lambda s: (s, 0, 0)),
+            whole(images, 3 * width, slots),
+            pl.BlockSpec((1, heads, 2 * slots), lambda s: (s, 0, 0)),
+            pl.BlockSpec((1, width, 2 * slots), lambda s: (s, 0, 0)),
+            pl.BlockSpec((2, slots, width), lambda s: (s // 2, 0, 0)),
+            whole(*all_three),
+            pl.BlockSpec((2, slots, width), lambda s: (s // 2, 0, 0)),
+            pl.BlockSpec((1, slots, width), lambda s: (s, 0, 0)),
+            whole(width, 3 * width),
+            whole(width, width),
+            *[pl.BlockSpec(memory_space=pl.ANY)] * share,
         ],
         out_specs=[
-            pl.BlockSpec((2, slots, width), lambda s, *_: (s // 2, 0, 0)),
-            pl.BlockSpec(all_three, lambda s, *_: (0, 0, 0), pipeline_mode=once),
-            pl.BlockSpec((width, 4 * width), lambda s, *_: (0, 0), pipeline_mode=once),
-            pl.BlockSpec((3 * width, 128), lambda s, *_: (0, 0), pipeline_mode=once),
+            pl.BlockSpec((2, slots, width), lambda s: (s // 2, 0, 0)),
+            whole(*all_three),
+            whole(width, 4 * width),
+            whole(3 * width, 128),
+            *[whole(*shape) for shape in shapes],
         ],
         scratch_shapes=[
-            pltpu.VMEM((2, 3 * width, slots), jnp.bfloat16),
-            pltpu.VMEM((images, 3 * width, slots), jnp.float32),
-            pltpu.VMEM(all_three, jnp.float32),
-            pltpu.VMEM((3 * width, width), jnp.float32),
-        ],
-    )
-    return pl.pallas_call(
-        attend_back_kernel,
-        grid_spec=grid_spec,
+            pltpu.VMEM((2, 3 * width, slots), low),
+            pltpu.VMEM((images, 3 * width, slots), wide),
+            pltpu.VMEM(all_three, wide),
+            pltpu.VMEM((3 * width, width), wide),
+            *[pltpu.VMEM(shape, wide) for shape in shapes],
+            *buffers,
+            *sems,
+        ],
         out_shape=[
-            jax.ShapeDtypeStruct((seqs, slots, width), jnp.float32),
-            jax.ShapeDtypeStruct(all_three, jnp.float32),
-            jax.ShapeDtypeStruct((width, 4 * width), jnp.bfloat16),
-            jax.ShapeDtypeStruct((3 * width, 128), jnp.float32),
-        ],
-        compiler_params=pltpu.CompilerParams(vmem_limit_bytes=48 * 1024 * 1024),
+            jax.ShapeDtypeStruct((seqs, slots, width), wide),
+            jax.ShapeDtypeStruct(all_three, wide),
+            jax.ShapeDtypeStruct((width, 4 * width), low),
+            jax.ShapeDtypeStruct((3 * width, 128), wide),
+            *[jax.ShapeDtypeStruct(shape, wide) for shape in shapes],
+        ],
+        compiler_params=pltpu.CompilerParams(vmem_limit_bytes=62 * 1024 * 1024, **params),
         name="attend_backward",
     )(lengths, counts, groups, cap_qkv, image_qkv, lse, context_grad, captions, regions, cap_sum,
-      region_sum, square, out_grad)
+      region_sum, square, out_grad, *partials)
 
 
 def on_device(
@@ -983,10 +1125,8 @@
     region_cotangent,
 ):
     width = captions.shape[2]
-    square, inner, outer, whole_vectors = gather_weights(
+    square, whole_vectors = gather_weights(
         (query_weight, key_weight, value_weight, out_weight),
-        inner_weight,
-        outer_weight,
         (
             query_bias,
             value_bias,
@@ -1017,9 +1157,13 @@
         axis=1,
     )
     scalars = (caption_lengths, seq_counts, group_ids)
-    cap_qkv, image_qkv, context, lse = attend_forward(
-        *scalars, captions, regions, square, bias_row
-    )
+    shards = (inner_weight, outer_weight)
+    cap_qkv, image_qkv, context, lse, *wholes = attend_forward(
+        *scalars, captions, regions, square, bias_row, shards if use_kernels else ()
+    )
+    if not use_kernels:
+        wholes = [lax.all_gather(shard, "fsdp", axis=0, tiled=True) for shard in shards]
+    inner, outer = wholes
     (
         out_caption,
         out_region,
@@ -1044,7 +1188,7 @@
         vectors,
         inner_all[None, :],
     )
-    grad_captions, grad_regions, square_grad, bias_wide = attend_backward(
+    grad_captions, grad_regions, square_grad, bias_wide, *totals = attend_backward(
         *scalars,
         cap_qkv,
         image_qkv,
@@ -1056,12 +1200,14 @@
         region_sum,
         square,
         out_grad,
-    )
+        (inner_grad, outer_grad) if use_kernels else (),
+    )
+    if not use_kernels:
+        totals = [reduce_native(part) for part in (inner_grad, outer_grad)]
+    inner_total, outer_total = totals
     bias_sums = jnp.sum(bias_wide, axis=1)
-    square_total, inner_total, outer_total, vector_totals = reduce_weights(
+    square_total, vector_totals = reduce_weights(
         square_grad,
-        inner_grad,
-        outer_grad,
         (
             bias_sums[:width],
             bias_sums[2 * width :],

time: 490 us -> 435 us (0.89)
  Pallas kernels: 465 us -> 406 us
    pallas_call x4, Pallas kernels: 319 us -> 260 us  [the longest x1 91.6 us: attend_backward(): pl.pallas_call(functools.partial(attend_back_kernel, share), grid=(seqs,)...]
    unnamed x32 -> x36, local copies, waits for them, and re-layouts: 11.3 us -> 14.3 us
where the time goes in v3:
time: 435 us; the launch traced here: 434 us
  Pallas kernels  406 us (93%)
  local copies, waits for them, and re-layouts  22.4 us (5%)
  other arithmetic  5.43 us (1%)
    pallas_call x1, Pallas kernels, feed_both(): pl.pallas_call(feed_kernel, grid_spec=grid_spec, out_shape=[jax.ShapeDtyp...  146 us
    pallas_call x1, Pallas kernels, attend_backward(): pl.pallas_call(functools.partial(attend_back_kernel, share), grid=(seqs,)...  91.6 us
    pallas_call x1, Pallas kernels, attend_forward(): pl.pallas_call(functools.partial(project_kernel, share), grid=(seqs,), in...  84.2 us
    pallas_call x1, Pallas kernels, reduce_all(): pl.pallas_call(functools.partial(reduce_kernel, splits, tile_rows(partial...  47.1 us
    pallas_call x1, Pallas kernels, gather_all(): pl.pallas_call(functools.partial(gather_kernel, splits, tile_rows(shards)...  36.7 us
    unnamed x36, local copies, waits for them, and re-layouts  14.3 us

profile of v3, /device:TPU:0, one launch (start us, length us, event | category | flops | bytes accessed | tf_op | source)
XLA Modules:
  0.0 434.4 jit_solution(4144658517728535548)
XLA Ops:
  0.7 1.7 pad_maximum_fusion.refs_0_
  2.4 0.7 reshape.150
  3.0 0.9 concatenate.14
  3.9 0.6 pad_convert_fusion
  4.5 36.7 %gather_rows.1 = (bf16[768,3072]{1,0:T(8,128)(2,1)}, f32[256,128]{1,0:T(8,128)}) custom-call(bf16[48,3072]{1,0:T(8,128)(2,1)} %pad_maximum_fusion.refs_0_, f32[16,128]{1,0:T(8,128)} %bitcast.29), custom_call_target="tpu_custom_call" | custom-call | tf_op jit(solution)/shard_map/gather_rows/pallas_call | solution.py:240
  41.2 0.9 reshape.156
  42.7 0.6 stack.7.vector_ref
  43.6 0.8 fusion.count_ref
  44.3 1.5 copy-done
  45.9 1.0 copy-done.2
  46.9 1.0 copy-done.4
  47.8 1.0 copy-done.5
  48.8 0.7 copy-done.7
  49.4 0.7 copy-done.8
  50.1 84.2 %attend_forward.1 = (bf16[10,2304,128]{2,1,0:T(8,128)(2,1)}, bf16[2,2304,128]{2,1,0:T(8,128)(2,1)S(1)}, bf16[10,768,256]{2,1,0:T(8,128)(2,1)}, f32[10,12,256]{2,...) custom-call(s32[10]{0:T(128)S(1)} %copy-done.7, s32[10]{0:T(128)S(1)} %fusion.count_ref, ...), custom_call_target="tpu_custom_call" | custom-call | tf_op jit(solution)/shard_map/attend_forward/pallas_call | solution.py:719
  134.4 1.0 copy-done.3
  135.4 0.7 copy-done.6
  136.1 0.7 broadcast_in_dim_reshape.3.inner_bias_ref
  136.8 146.2 %feed_both.1 = (bf16[10,128,768]{2,1,0:T(8,128)(2,1)}, bf16[10,128,768]{2,1,0:T(8,128)(2,1)}, f32[10,128,768]{2,1,0:T(8,128)}, f32[10,128,768]{2,1,0:T(8,128)}, ...) custom-call(s32[10]{0:T(128)} %length_ref.5, ...), custom_call_target="tpu_custom_call" | custom-call | tf_op jit(solution)/shard_map/feed_both/pallas_call | solution.py:911
  283.1 91.6 %attend_backward.1 = (f32[10,128,768]{2,1,0:T(8,128)}, f32[2,128,768]{2,1,0:T(8,128)}, bf16[768,3072]{1,0:T(8,128)(2,1)}, f32[2304,128]{1,0:T(8,128)}, f32[48,3072]{1,0:T(8,128)}, /*index=5*/f32[192,768]{1,0:T(8,128)}) custom-call(s32[10]{0:T(128)} %length_ref.5, s32[10]{0:T(128)} %copy-done.9, s32[10]{0:T(128)} %group_ref.5, ...), custom_call_target="tpu_custom_call" | custom-call | tf_op jit(solution)/shard_map/attend_backward/pallas_call | solution.py:1056
  374.6 1.6 reduce_sum.19
  377.0 0.5 broadcast.15
  377.5 0.7 reduce.15
  378.4 2.3 copy-done.1
  380.8 47.1 %reduce_rows.1 = (f32[48,3072]{1,0:T(8,128)S(1)}, f32[16,128]{1,0:T(8,128)S(1)}) custom-call(bf16[768,3072]{1,0:T(8,128)(2,1)S(1)} %copy-done.1, f32[256,128]{1,0:T(8,128)S(1)} %reshape.161.refs_1_), custom_call_target="tpu_custom_call" | custom-call | tf_op jit(solution)/shard_map/reduce_rows/pallas_call | solution.py:490
  427.8 0.8 fusion.1
  428.7 0.6 slice_bitcast_fusion
  429.3 0.6 slice.136
  429.9 2.0 copy.45
  431.9 0.9 copy.46
  432.8 0.8 copy.47
  433.6 0.8 copy.48
  (51 shorter events, 1.7 us)
Async XLA Ops:
  44.3 1.5 copy-start
  45.9 1.0 copy-start.2
  46.9 1.0 copy-start.4
  47.8 1.0 copy-start.5
  48.8 0.7 copy-start.7
  49.4 0.7 copy-start.8
  50.1 86.7 %copy-start.9 = (s32[10]{0:T(128)}, s32[10]{0:T(128)S(1)}, u32[]{:S(2)}) copy-start(s32[10]{0:T(128)S(1)} %fusion.count_ref) | copy-start | bytes 124
  134.4 1.0 copy-start.3
  135.4 0.7 copy-start.6
  283.0 93.4 %copy-start.14 = (f32[8,768]{1,0:T(8,128)S(1)}, f32[8,768]{1,0:T(8,128)}, u32[]{:S(2)}) copy-start(f32[8,768]{1,0:T(8,128)} %get-tuple-element.65) | copy-start | bytes 73732
  283.0 94.5 %copy-start.15 = (f32[1,3072]{1,0:T(1,128)S(1)}, f32[1,3072]{1,0:T(1,128)}, u32[]{:S(2)}) copy-start(f32[1,3072]{1,0:T(1,128)} %get-tuple-element.66) | copy-start | bytes 36868
  378.4 2.3 copy-start.1
  380.8 49.2 %copy-start.10 = (f32[10,128,768]{2,1,0:T(8,128)S(1)}, f32[10,128,768]{2,1,0:T(8,128)}, u32[]{:S(2)}) copy-start(f32[10,128,768]{2,1,0:T(8,128)} %get-tuple-element.120) | copy-start | bytes 11796484
  429.9 2.0 copy-start.11
  429.9 2.9 copy-start.13
  429.9 3.7 copy-start.12
